TPU v7x, 32 devices: a whole 2x2x4 slice. The times are simulated.
32 devices in a mesh: gx: 8 (over z, x), gy: 4 (over y, core).
Axes of the slice: x: 2, y: 2, z: 4, core: 2. Of those that a mesh axis runs over, the one named last changes fastest.
Arguments:
- initial_guess_field: float32 [2, 2, 512, 2048], P(None, None, 'gx', 'gy'), may hold values from -18 to 18
- medium_label: int32 [512, 2048], P('gx', 'gy'), may hold values from 0 to 3
- principal_entry_addend: float32 [4, 2], replicated, may hold values from -0.5 to 0.8, as said below
- linearized_block_weight: float32 [25, 4, 2], replicated, may hold values from -1.25 to 1.25
- sample_abscissae: float32 [24, 2], replicated, may hold values from -1 to 1
- singularity_locations: float32 [24, 2], replicated, may hold values from -1 to 6, as said below
- basis_normalizers: float32 [24], replicated, may hold values from 0.8 to 1.6
- spectral_target: float32 [2], replicated, may hold values from -0.5 to 0.5
- quasi_periodic_phase: float32 [2, 2], replicated, may hold values from -3.140625 to 3.140625
Outputs:
- basis: float32 [2, 3, 2, 512, 2048], P(None, None, None, 'gx', 'gy')
- hessenberg: float32 [2, 2, 4, 3], replicated
Inputs may be any that keep to these rules, and one draw needn't show every extreme that they name: `principal_entry_addend`: real parts lie in 0.2 to 0.8, imaginary parts in -0.5 to 0.5. `singularity_locations`: real parts lie in 3 to 6, imaginary parts in -1 to 1.
All inputs are finite; a program needn't handle non-finite values.
Results may differ from a plain program's by a relative error of at most 0.0003.
Values sent between devices are 32-bit elements; how exact they have to be, the bound alone decides.
No kernel may reach another device: no remote copies, remote signals or barrier semaphores. Data moves between devices by JAX's collectives and lax.ppermute only.
A program may use at most 128 MiB of HBM per device.

v0:
```python
import jax
import jax.numpy as jnp
from jax import lax
from jax.sharding import PartitionSpec as P

STEPS = 3
SWEEPS = 4


HIGHEST = lax.Precision.HIGHEST


def padded_2(block, sides, width):
    for axis, dim in sides:
        count = lax.axis_size(axis)
        forward = [(i, i + 1) for i in range(count - 1)]
        forward.append((count - 1, 0))
        backward = [(target, source) for source, target in forward]
        low = lax.ppermute(
            lax.slice_in_dim(block, block.shape[dim] - width, None, axis=dim), axis, forward
        )
        high = lax.ppermute(lax.slice_in_dim(block, 0, width, axis=dim), axis, backward)
        block = jnp.concatenate([low, block, high], axis=dim)
    return block


def fraction_weights(sample_abscissae, singularity_locations, basis_normalizers, spectral_target):
    gap_real = spectral_target[0] - sample_abscissae[:, 0]
    gap_imag = spectral_target[1] - sample_abscissae[:, 1]
    pole_size = (
        singularity_locations[:, 0] * singularity_locations[:, 0]
        + singularity_locations[:, 1] * singularity_locations[:, 1]
    )
    quotient_inphase = (
        spectral_target[0] * singularity_locations[:, 0]
        + spectral_target[1] * singularity_locations[:, 1]
    ) / pole_size
    quotient_quadrature = (
        spectral_target[1] * singularity_locations[:, 0]
        - spectral_target[0] * singularity_locations[:, 1]
    ) / pole_size
    subordinate_inphase = basis_normalizers * (1.0 - quotient_inphase)
    subordinate_quadrature = -basis_normalizers * quotient_quadrature
    lower_size = (
        subordinate_inphase * subordinate_inphase + subordinate_quadrature * subordinate_quadrature
    )
    multiplier_inphase = (
        gap_real * subordinate_inphase + gap_imag * subordinate_quadrature
    ) / lower_size
    multiplier_quadrature = (
        gap_imag * subordinate_inphase - gap_real * subordinate_quadrature
    ) / lower_size
    return (multiplier_inphase, multiplier_quadrature)


def cell_inverse(onehot, principal_entry_addend):
    shifted = jnp.einsum("mxy,mc->cxy", onehot, principal_entry_addend, precision=HIGHEST)
    center = 4.0 + shifted[0]
    size_sq = center * center + shifted[1] * shifted[1]
    return jnp.stack([center / size_sq, -shifted[1] / size_sq])


def times_inverse(grid_field, inverse):
    real_part = grid_field[:, 0] * inverse[0] - grid_field[:, 1] * inverse[1]
    imag_part = grid_field[:, 0] * inverse[1] + grid_field[:, 1] * inverse[0]
    return jnp.stack([real_part, imag_part], 1)


def neighbours(padded):
    return (
        padded[:, :, 2:, 1:-1]
        + padded[:, :, :-2, 1:-1]
        + padded[:, :, 1:-1, 2:]
        + padded[:, :, 1:-1, :-2]
    )


def rotate(padded, angles, row_sign, column_sign):
    phase_angle = (
        row_sign[None, :, None] * angles[:, 0][:, None, None]
        + column_sign[None, None, :] * angles[:, 1][:, None, None]
    )
    cosine = jnp.cos(phase_angle)
    sine_part = jnp.sin(phase_angle)
    real_part = padded[:, 0] * cosine - padded[:, 1] * sine_part
    imag_part = padded[:, 0] * sine_part + padded[:, 1] * cosine
    return jnp.stack([real_part, imag_part], 1)


def body_twist(padded, angles, margin):
    row_count = padded.shape[2]
    column_count = padded.shape[3]
    row_positions = jnp.arange(row_count)
    column_positions = jnp.arange(column_count)
    low_rows = lax.axis_index("gx") == 0
    high_rows = lax.axis_index("gx") == lax.axis_size("gx") - 1
    low_columns = lax.axis_index("gy") == 0
    high_columns = lax.axis_index("gy") == lax.axis_size("gy") - 1
    row_sign = jnp.where(low_rows & (row_positions < margin), -1.0, 0.0) + jnp.where(
        high_rows & (row_positions >= row_count - margin), 1.0, 0.0
    )
    column_sign = jnp.where(low_columns & (column_positions < margin), -1.0, 0.0) + jnp.where(
        high_columns & (column_positions >= column_count - margin), 1.0, 0.0
    )
    return rotate(padded, angles, row_sign.astype(jnp.float32), column_sign.astype(jnp.float32))


def right_side(vectors_now, current, linearized_block_weight, onehot):
    mixing_real = jnp.einsum(
        "bm,kbc->kmc", linearized_block_weight[:, :, 0], current[:, :, 0], precision=HIGHEST
    ) - jnp.einsum(
        "bm,kbc->kmc", linearized_block_weight[:, :, 1], current[:, :, 1], precision=HIGHEST
    )
    mixing_imag = jnp.einsum(
        "bm,kbc->kmc", linearized_block_weight[:, :, 0], current[:, :, 1], precision=HIGHEST
    ) + jnp.einsum(
        "bm,kbc->kmc", linearized_block_weight[:, :, 1], current[:, :, 0], precision=HIGHEST
    )
    cell_real = jnp.einsum("kmc,mxy->kcxy", mixing_real, onehot, precision=HIGHEST)
    cell_imag = jnp.einsum("kmc,mxy->kcxy", mixing_imag, onehot, precision=HIGHEST)
    real_part = jnp.sum(cell_real * vectors_now[:, :, 0] - cell_imag * vectors_now[:, :, 1], axis=1)
    imag_part = jnp.sum(cell_real * vectors_now[:, :, 1] + cell_imag * vectors_now[:, :, 0], axis=1)
    return jnp.stack([real_part, imag_part], 1)


def grid_inner(vectors_now, grid_field):
    inner_real = jnp.einsum(
        "kcxy,kxy->kc", vectors_now[:, :, 0], grid_field[:, 0], precision=HIGHEST
    ) + jnp.einsum("kcxy,kxy->kc", vectors_now[:, :, 1], grid_field[:, 1], precision=HIGHEST)
    inner_imag = jnp.einsum(
        "kcxy,kxy->kc", vectors_now[:, :, 0], grid_field[:, 1], precision=HIGHEST
    ) - jnp.einsum("kcxy,kxy->kc", vectors_now[:, :, 1], grid_field[:, 0], precision=HIGHEST)
    return (inner_real, inner_imag)


def grid_remove(vectors_now, grid_field, inner_real, inner_imag):
    real_part = grid_field[:, 0] - (
        jnp.einsum("kc,kcxy->kxy", inner_real, vectors_now[:, :, 0], precision=HIGHEST)
        - jnp.einsum("kc,kcxy->kxy", inner_imag, vectors_now[:, :, 1], precision=HIGHEST)
    )
    imag_part = grid_field[:, 1] - (
        jnp.einsum("kc,kcxy->kxy", inner_real, vectors_now[:, :, 1], precision=HIGHEST)
        + jnp.einsum("kc,kcxy->kxy", inner_imag, vectors_now[:, :, 0], precision=HIGHEST)
    )
    return jnp.stack([real_part, imag_part], 1)


def block_chain(coords_real, coords_imag, current_full, multiplier_inphase, multiplier_quadrature):
    blockwise = [jnp.stack([coords_real, coords_imag], 1)]
    for block_id in range(current_full.shape[1] - 1):
        previous = blockwise[-1]
        real_part = (
            multiplier_inphase[block_id] * previous[:, 0]
            - multiplier_quadrature[block_id] * previous[:, 1]
            + current_full[:, block_id + 1, 0]
        )
        imag_part = (
            multiplier_inphase[block_id] * previous[:, 1]
            + multiplier_quadrature[block_id] * previous[:, 0]
            + current_full[:, block_id + 1, 1]
        )
        blockwise.append(jnp.stack([real_part, imag_part], 1))
    return jnp.stack(blockwise, 1)


def level_inner(older, newer):
    inner_real = jnp.einsum(
        "kcbr,kbr->kc", older[:, :, :, 0], newer[:, :, 0], precision=HIGHEST
    ) + jnp.einsum("kcbr,kbr->kc", older[:, :, :, 1], newer[:, :, 1], precision=HIGHEST)
    inner_imag = jnp.einsum(
        "kcbr,kbr->kc", older[:, :, :, 0], newer[:, :, 1], precision=HIGHEST
    ) - jnp.einsum("kcbr,kbr->kc", older[:, :, :, 1], newer[:, :, 0], precision=HIGHEST)
    return (inner_real, inner_imag)


def level_remove(older, newer, inner_real, inner_imag):
    real_part = newer[:, :, 0] - (
        jnp.einsum("kc,kcbr->kbr", inner_real, older[:, :, :, 0], precision=HIGHEST)
        - jnp.einsum("kc,kcbr->kbr", inner_imag, older[:, :, :, 1], precision=HIGHEST)
    )
    imag_part = newer[:, :, 1] - (
        jnp.einsum("kc,kcbr->kbr", inner_real, older[:, :, :, 1], precision=HIGHEST)
        + jnp.einsum("kc,kcbr->kbr", inner_imag, older[:, :, :, 0], precision=HIGHEST)
    )
    return jnp.stack([real_part, imag_part], 2)


def level_step(coeffs, hessen, blockwise, active, section_id):
    older = coeffs[:, :active]
    first_real, first_imag = level_inner(older, blockwise)
    orthog_once = level_remove(older, blockwise, first_real, first_imag)
    second_real, second_imag = level_inner(older, orthog_once)
    orthog_twice = level_remove(older, orthog_once, second_real, second_imag)
    length = jnp.sqrt(jnp.sum(orthog_twice * orthog_twice, axis=(1, 2, 3)))
    coeffs = coeffs.at[:, active].set(orthog_twice / length[:, None, None, None])
    hessen = hessen.at[:, 0, :active, section_id].set(first_real + second_real)
    hessen = hessen.at[:, 1, :active, section_id].set(first_imag + second_imag)
    hessen = hessen.at[:, 0, active, section_id].set(length)
    return (coeffs, hessen)


def per_device(
    initial_guess_field,
    medium_label,
    principal_entry_addend,
    linearized_block_weight,
    sample_abscissae,
    singularity_locations,
    basis_normalizers,
    spectral_target,
    quasi_periodic_phase,
):
    materials = principal_entry_addend.shape[0]
    points = initial_guess_field.shape[0]
    blocks = linearized_block_weight.shape[0]
    rank_count = STEPS + 1
    onehot = (medium_label[None] == jnp.arange(materials, dtype=jnp.int32)[:, None, None]).astype(
        jnp.float32
    )
    inverse = cell_inverse(onehot, principal_entry_addend)
    multiplier_inphase, multiplier_quadrature = fraction_weights(
        sample_abscissae, singularity_locations, basis_normalizers, spectral_target
    )
    squares = jnp.sum(initial_guess_field * initial_guess_field, axis=(1, 2, 3))
    scale_start = jnp.sqrt(lax.psum(squares, ("gx", "gy")))
    vectors = [initial_guess_field / scale_start[:, None, None, None]]
    coeffs = (
        jnp.zeros((points, rank_count, blocks, 2, rank_count), jnp.float32)
        .at[:, 0, 0, 0, 0]
        .set(1.0)
    )
    hessen = jnp.zeros((points, 2, rank_count, STEPS), jnp.float32)
    for section_id in range(STEPS):
        active = section_id + 1
        vectors_now = jnp.stack(vectors, 1)
        source = right_side(
            vectors_now, coeffs[:, section_id, :, :, :active], linearized_block_weight, onehot
        )
        solved = times_inverse(source, inverse)
        for repeat in range(SWEEPS):
            padded = padded_2(solved, (("gx", 2), ("gy", 3)), 1)
            padded = body_twist(padded, quasi_periodic_phase, 1)
            solved = times_inverse(source + neighbours(padded), inverse)
        part_real, part_imag = grid_inner(vectors_now, solved)
        part_square = jnp.sum(solved * solved, axis=(1, 2, 3))
        inner_real, inner_imag, whole_square = lax.psum(
            (part_real, part_imag, part_square), ("gx", "gy")
        )
        orthog_once = grid_remove(vectors_now, solved, inner_real, inner_imag)
        length = jnp.sqrt(
            whole_square - jnp.sum(inner_real * inner_real + inner_imag * inner_imag, axis=1)
        )
        vectors.append(orthog_once / length[:, None, None, None])
        coords_real = (
            jnp.zeros((points, rank_count), jnp.float32)
            .at[:, :active]
            .set(inner_real)
            .at[:, active]
            .set(length)
        )
        coords_imag = jnp.zeros((points, rank_count), jnp.float32).at[:, :active].set(inner_imag)
        blockwise = block_chain(
            coords_real,
            coords_imag,
            coeffs[:, section_id],
            multiplier_inphase,
            multiplier_quadrature,
        )
        coeffs, hessen = level_step(coeffs, hessen, blockwise, active, section_id)
    return (jnp.stack(vectors[1:], 1), hessen)


def solution(mesh):
    return jax.shard_map(
        per_device,
        mesh=mesh,
        in_specs=(P(None, None, "gx", "gy"), P("gx", "gy"), P(), P(), P(), P(), P(), P(), P()),
        out_specs=(P(None, None, None, "gx", "gy"), P()),
        check_vma=False,
    )
```

profile of v0, /device:TPU:0, one launch (start us, length us, event | category | flops | bytes accessed | tf_op | source)
XLA Modules:
  0.0 701.8 jit_solution(3626380374497232272)
XLA Ops:
  7.6 41.9 %psum.70 = f32[2]{0:T(128)S(1)} all-reduce(f32[2]{0:T(128)S(1)} %multiply_reduce_fusion), channel_id=1, replica_groups=mesh['gx'=8,'gy'=4] {'gx','gy'}, use_global_device_ids=true, to_apply=%region_1.0 | all-reduce | flops 2 | bytes 16 | tf_op jit(solution)/shard_map/psum | solution.py:225
  64.6 5.5 fusion.165
  86.2 5.5 fusion.167
  107.5 5.5 fusion.169
  128.9 5.5 fusion.171
  139.6 40.9 %all-reduce.8 = (f32[2,1]{0,1:T(1,128)S(1)}, f32[2,1]{0,1:T(1,128)S(1)}, f32[2]{0:T(128)S(1)}) all-reduce(f32[2,1]{0,1:T(1,128)S(1)} %subtract_bitcast_fusion.5, f32[2,1]{0,1:T(1,128)S(1)} %add_bitcast_fusion.7, f32[2]{0:T(128)S(1)} %fusion.109), channel_id=1, replica_groups=mesh['gx'=8,'gy'=4] {'gx','gy'}, use_global_device_ids=true, to_apply=%region_3.0 | all-reduce | flops 6 | bytes 48 | tf_op jit(solution)/shard_map/psum | solution.py:246
  182.5 29.7 %multiply_subtract_fusion.15 = (f32[2,4]{0,1:T(4,128)S(1)}, f32[2,4]{0,1:T(4,128)S(1)}, f32[2,4]{0,1:T(4,128)S(1)}, f32[2,4]{0,1:T(4,128)S(1)}, f32[2,4]{0,1:T(4...) fusion(f32[]{:T(128)} %bitcast.148, ...), kind=kLoop, calls=%fused_computation.778 | loop fusion | flops 1128 | bytes 1736 | tf_op jit(solution)/shard_map/sub | solution.py:153
  238.6 5.5 fusion.173
  259.8 5.5 fusion.175
  281.2 5.5 fusion.177
  305.5 5.5 fusion.179
  319.4 4.9 fusion.215
  324.3 4.9 fusion.211
  329.2 5.3 fusion.209
  335.6 38.3 %all-reduce.7 = (f32[2,2]{0,1:T(2,128)S(1)}, f32[2,2]{0,1:T(2,128)S(1)}, f32[2]{0:T(128)S(1)}) all-reduce(f32[2,2]{0,1:T(2,128)S(1)} %bitcast_subtract_fusion.7, f32[2,2]{0,1:T(2,128)S(1)} %bitcast_add_fusion.99, f32[2]{0:T(128)S(1)} %fusion.110), channel_id=1, replica_groups=mesh['gx'=8,'gy'=4] {'gx','gy'}, use_global_device_ids=true, to_apply=%region_12.13 | all-reduce | flops 10 | bytes 80 | tf_op jit(solution)/shard_map/psum | solution.py:246
  375.5 29.8 %bitcast_add_fusion.52 = (f32[2,4]{0,1:T(4,128)S(1)}, f32[2,4]{0,1:T(4,128)S(1)}, f32[2,4]{0,1:T(4,128)S(1)}, f32[2,4]{0,1:T(4,128)S(1)}, f32[2,4]{0,1:T(4,128)S...) fusion(f32[2,1,1,4]{0,3,2,1:T(4,128)S(1)} %copy.2232, ...), kind=kLoop, calls=%fused_computation.729 | loop fusion | flops 1504 | bytes 3248 | tf_op jit(solution)/shard_map/add | solution.py:153
  450.0 5.5 fusion.181
  471.5 5.5 fusion.183
  492.9 5.5 fusion.185
  574.1 5.5 fusion.187
  592.8 4.9 fusion.12
  598.1 5.0 fusion.10
  604.8 38.3 %all-reduce.6 = (f32[2,3]{0,1:T(4,128)S(1)}, f32[2,3]{0,1:T(4,128)S(1)}, f32[2]{0:T(128)S(1)}) all-reduce(f32[2,3]{0,1:T(4,128)S(1)} %bitcast_subtract_fusion.6, f32[2,3]{0,1:T(4,128)S(1)} %bitcast_add_fusion.50, f32[2]{0:T(128)S(1)} %fusion.111), channel_id=1, replica_groups=mesh['gx'=8,'gy'=4] {'gx','gy'}, use_global_device_ids=true, to_apply=%region_22.23 | all-reduce | flops 14 | bytes 112 | tf_op jit(solution)/shard_map/psum | solution.py:246
  643.6 29.8 %bitcast_add_fusion.3 = (f32[2,4]{0,1:T(4,128)S(1)}, f32[2,4]{0,1:T(4,128)S(1)}, f32[2,4]{0,1:T(4,128)S(1)}, f32[2,4]{0,1:T(4,128)S(1)}, f32[2,4]{0,1:T(4,128)S(...) fusion(f32[2,1,1,4]{0,3,2,1:T(4,128)S(1)} %copy-done.46, ...), kind=kLoop, calls=%fused_computation.679 | loop fusion | flops 1512 | bytes 3288 | tf_op jit(solution)/shard_map/add | solution.py:153
  (896 shorter events, 359.0 us)
Async XLA Ops:
  51.3 6.4 collective-permute-start
  58.0 5.7 collective-permute-start.3
  72.8 6.4 collective-permute-start.4
  94.3 6.5 collective-permute-start.8
  94.4 6.4 collective-permute-start.9
  115.6 6.5 collective-permute-start.12
  115.7 6.4 collective-permute-start.13
  225.4 6.4 collective-permute-start.16
  232.0 5.7 collective-permute-start.19
  246.7 6.4 collective-permute-start.20
  267.9 6.5 collective-permute-start.24
  268.0 6.4 collective-permute-start.25
  289.3 9.2 %collective-permute-start.28 = (f32[2,2,1,512]{3,0,2,1:T(2,128)S(1)}, f32[2,2,1,512]{3,0,2,1:T(2,128)S(1)}, u32[]{:S(2)}, u32[]{:S(2)}) collective-permute-start(f32[2,2,1,512]{3,0,2,1:T(2,128)S(1)} %get-tuple-element.567), channel_id=1, source_target_pairs={{0,4},{4,8},{8,12},{12,16},{16,20},{20,24},{24,28},{28,0},{1,5},{5... | collective-permute-start | bytes 24584 | tf_op jit(solution)/shard_map/ppermute | solution.py:19
  289.4 9.1 %collective-permute-start.29 = (f32[2,2,1,512]{3,0,2,1:T(2,128)S(1)}, f32[2,2,1,512]{3,0,2,1:T(2,128)S(1)}, u32[]{:S(2)}, u32[]{:S(2)}) collective-permute-start(f32[2,2,1,512]{3,0,2,1:T(2,128)S(1)} %get-tuple-element.568), channel_id=1, source_target_pairs={{4,0},{8,4},{12,8},{16,12},{20,16},{24,20},{28,24},{0,28},{5,1},{9... | collective-permute-start | bytes 24584 | tf_op jit(solution)/shard_map/ppermute | solution.py:22
  436.7 6.4 collective-permute-start.32
  443.4 5.7 collective-permute-start.35
  458.1 6.4 collective-permute-start.36
  465.0 5.5 collective-permute-start.39
  479.6 6.5 collective-permute-start.40
  479.8 6.3 collective-permute-start.41
  502.4 55.5 %collective-permute-start.44 = (f32[2,2,1,512]{3,0,2,1:T(2,128)}, f32[2,2,1,512]{3,0,2,1:T(2,128)S(1)}, u32[]{:S(2)}, u32[]{:S(2)}) collective-permute-start(f32[2,2,1,512]{3,0,2,1:T(2,128)} %get-tuple-element.559), channel_id=1, source_target_pairs={{0,4},{4,8},{8,12},{12,16},{16,20},{20,24},{24,28},{28,0},{1,5},{5... | collective-permute-start | bytes 24584 | tf_op jit(solution)/shard_map/ppermute | solution.py:19
  502.4 55.4 %collective-permute-start.45 = (f32[2,2,1,512]{3,0,2,1:T(2,128)}, f32[2,2,1,512]{3,0,2,1:T(2,128)S(1)}, u32[]{:S(2)}, u32[]{:S(2)}) collective-permute-start(f32[2,2,1,512]{3,0,2,1:T(2,128)} %get-tuple-element.560), channel_id=1, source_target_pairs={{4,0},{8,4},{12,8},{16,12},{20,16},{24,20},{28,24},{0,28},{5,1},{9... | collective-permute-start | bytes 24584 | tf_op jit(solution)/shard_map/ppermute | solution.py:22
  559.7 12.4 %collective-permute-start.46 = (f32[2,2,66,1]{3,0,2,1:T(2,128)}, f32[2,2,66,1]{3,0,2,1:T(2,128)}, u32[]{:S(2)}, u32[]{:S(2)}) collective-permute-start(f32[2,2,66,1]{3,0,2,1:T(2,128)} %get-tuple-element.533), channel_id=1, source_target_pairs={{0,1},{1,2},{2,3},{3,0},{4,5},{5,6},{6,7},{7,4},{8,9},{9,10},{10,1... | collective-permute-start | bytes 3176 | tf_op jit(solution)/shard_map/ppermute | solution.py:19
  560.6 11.4 %collective-permute-start.47 = (f32[2,2,66,1]{3,0,2,1:T(2,128)}, f32[2,2,66,1]{3,0,2,1:T(2,128)}, u32[]{:S(2)}, u32[]{:S(2)}) collective-permute-start(f32[2,2,66,1]{3,0,2,1:T(2,128)} %get-tuple-element.534), channel_id=1, source_target_pairs={{1,0},{2,1},{3,2},{0,3},{5,4},{6,5},{7,6},{4,7},{9,8},{10,9},{11,1... | collective-permute-start | bytes 3176 | tf_op jit(solution)/shard_map/ppermute | solution.py:22
  (90 other events, 2244.9 us)
where the time goes:
time: 712 us; the launch traced here: 702 us
  other arithmetic  231 us (32%)
  blocking collectives  159 us (22%)
  local copies, waits for them, and re-layouts  103 us (14%)
  starting transfers between devices  81.1 us (11%)
  matrix products  80.5 us (11%)
  waiting for transfers between devices  43.5 us (6%)
    psum x3, blocking collectives, per_device(): lax.psum((part_real, part_imag, part_square), ('gx', 'gy'))  117 us
    add x12, other arithmetic, rotate(): imag_part = padded[:, 0] * sine_part + padded[:, 1] * cosine  65.8 us
    ppermute x24, starting transfers between devices, padded_2(): lax.ppermute(lax.slice_in_dim(block, 0, width, axis=dim), axis, backward)  62.9 us
    add x2, other arithmetic, block_chain(): multiplier_inphase[block_id] * previous[:, 0]  59.6 us
    psum x1, blocking collectives, per_device(): scale_start = jnp.sqrt(lax.psum(squares, ('gx', 'gy')))  41.9 us
    squeeze x48, local copies, waits for them, and re-layouts, block_chain(): current_full[:, block_id + 1, 0]  33.2 us
    squeeze x48, local copies, waits for them, and re-layouts, block_chain(): current_full[:, block_id + 1, 1]  31.5 us
    ppermute x24, waiting for transfers between devices, padded_2(): lax.ppermute(lax.slice_in_dim(block, block.shape[dim] - width, None, axis...  29.9 us
  transfers between devices with their start and end apart: 48, of which 32 were waited for; matrix products, arithmetic and copies ran while one was open for 11% of the time, Pallas kernels for 0%

commit v1 on v0

v1 whole, which is shorter than its diff:
```python
import functools

import jax
import jax.numpy as jnp
from jax import lax
from jax.experimental import pallas as pl
from jax.experimental.pallas import tpu as pltpu
from jax.sharding import PartitionSpec as P

STEPS = 3
SWEEPS = 4
HALO = STEPS * SWEEPS
LANES = 128
SUB = 8
SLOT = 16
F32 = jnp.float32
VMEM = pl.BlockSpec(memory_space=pltpu.VMEM)
SMEM = pl.BlockSpec(memory_space=pltpu.SMEM)
ANY = pl.BlockSpec(memory_space=pl.ANY)
MIB = 1024 * 1024


def even(axis):
    return lax.rem(lax.axis_index(axis), 2) == 0


def swap_near(axis):
    return [(i, i ^ 1) for i in range(lax.axis_size(axis))]


def swap_far(axis):
    n = lax.axis_size(axis)
    return [(i, (i + 1) % n if i % 2 else (i - 1) % n) for i in range(n)]


def cmul(a, b):
    return (a[0] * b[0] - a[1] * b[1], a[0] * b[1] + a[1] * b[0])


def cadd(a, b):
    return (a[0] + b[0], a[1] + b[1])


def csub(a, b):
    return (a[0] - b[0], a[1] - b[1])


def conj_mul(a, b):
    return (a[0] * b[0] + a[1] * b[1], a[0] * b[1] - a[1] * b[0])


def pack_rows(z_ref, m_ref, near_ref, far_ref):
    points, _, rows, _ = z_ref.shape
    is_even = even("gx")
    for plane in range(2 * points + 1):
        if plane < 2 * points:
            top = z_ref[plane // 2, plane % 2, 0:HALO, :]
            bottom = z_ref[plane // 2, plane % 2, rows - HALO : rows, :]
        else:
            top = m_ref[0:HALO, :].astype(F32)
            bottom = m_ref[rows - HALO : rows, :].astype(F32)
        span = slice(plane * HALO, (plane + 1) * HALO)
        near_ref[span, :] = jnp.where(is_even, bottom, top)
        far_ref[span, :] = jnp.where(is_even, top, bottom)


def params(a_ref, w_ref, node_ref, pole_ref, scale_ref, target_ref, phase_ref,
           table_ref, trig_ref, chain_ref, size_ref):
    shape = (SUB, LANES)

    def splat(value):
        return jnp.full(shape, value, F32)

    mats = a_ref.shape[0]
    totals = node_ref.shape[0]
    target = (splat(target_ref[0]), splat(target_ref[1]))
    steps = []
    for j in range(totals):
        gap = csub(target, (splat(node_ref[j, 0]), splat(node_ref[j, 1])))
        pole = (splat(pole_ref[j, 0]), splat(pole_ref[j, 1]))
        pole_size = pole[0] * pole[0] + pole[1] * pole[1]
        quotient = conj_mul(pole, target)
        quotient = (quotient[0] / pole_size, quotient[1] / pole_size)
        scale = splat(scale_ref[j])
        lower = (scale * (1.0 - quotient[0]), -scale * quotient[1])
        size = lower[0] * lower[0] + lower[1] * lower[1]
        factor = conj_mul(lower, gap)
        steps.append((factor[0] / size, factor[1] / size))
    zero = jnp.zeros(shape, F32)
    power = (splat(1.0), zero)
    size = splat(1.0)
    sums = [zero[:mats, :2]] * 4
    for b in range(totals + 1):
        if b > 0:
            power = cmul(power, steps[b - 1])
            size = size + power[0] * power[0] + power[1] * power[1]
        w = w_ref[b]
        pr = power[0][:mats, :2]
        pi = power[1][:mats, :2]
        sums[0] = sums[0] + w * pr
        sums[1] = sums[1] + w * pi
        sums[2] = sums[2] + float(b) * (w * pr)
        sums[3] = sums[3] + float(b) * (w * pi)
    gamma = jnp.sqrt(size)
    size_ref[...] = gamma

    def full(value):
        return jnp.broadcast_to(value, shape)

    for m in range(mats):
        center = 4.0 + splat(a_ref[m, 0])
        side = splat(a_ref[m, 1])
        lower = center * center + side * side
        inverse = (center / lower, -side / lower)
        first = (full(w_ref[0, m : m + 1, 0:1]), full(w_ref[0, m : m + 1, 1:2]))
        parts = [[full(s[m : m + 1, c : c + 1]) for c in range(2)] for s in sums]
        a_weight = (parts[0][0] - parts[1][1], parts[0][1] + parts[1][0])
        b_weight = (parts[2][0] - parts[3][1], parts[2][1] + parts[3][0])
        a_weight = (a_weight[0] / gamma, a_weight[1] / gamma)
        b_weight = (b_weight[0] / gamma / gamma, b_weight[1] / gamma / gamma)
        entries = (inverse, cmul(inverse, first), cmul(inverse, a_weight), cmul(inverse, b_weight))
        for e, (re, im) in enumerate(entries):
            table_ref[2 * e, m] = re
            table_ref[2 * e + 1, m] = im
    for k in range(phase_ref.shape[0]):
        for axis in range(2):
            angle = splat(phase_ref[k, axis])
            trig_ref[k, axis, 0] = jnp.cos(angle)
            trig_ref[k, axis, 1] = jnp.sin(angle)
    depth = chain_ref.shape[2]
    row = lax.broadcasted_iota(jnp.int32, shape, 0)
    tiles = [[], []]
    for c in range(2):
        for t in range(depth // SUB):
            value = zero
            for r in range(SUB):
                b = t * SUB + r
                if 1 <= b <= totals:
                    value = jnp.where(row == r, steps[b - 1][c], value)
            tiles[c].append(value)
    step = tuple(jnp.concatenate(tile, 0) for tile in tiles)
    for s in range(chain_ref.shape[0]):
        chain_ref[s, 0] = step[0]
        chain_ref[s, 1] = step[1]
        moved = (pltpu.roll(step[0], 1 << s, 0), pltpu.roll(step[1], 1 << s, 0))
        step = cmul(step, moved)


def pack_columns(z_ref, m_ref, near_ref, far_ref, trig_ref, full_ref, near_out, far_out):
    points, _, rows, columns = z_ref.shape
    tiles = columns // LANES
    planes = 2 * points + 1
    total = rows + 2 * HALO
    is_even = even("gx")
    first = lax.axis_index("gx") == 0
    last = lax.axis_index("gx") == lax.axis_size("gx") - 1
    row = lax.broadcasted_iota(jnp.int32, (2 * HALO, LANES), 0)
    for plane in range(planes):
        span = slice(plane * HALO, (plane + 1) * HALO)
        for t in range(tiles):
            lanes = slice(t * LANES, (t + 1) * LANES)
            if plane < 2 * points:
                full_ref[plane, t, 0:rows, :] = z_ref[plane // 2, plane % 2, :, lanes]
            else:
                full_ref[plane, t, 0:rows, :] = m_ref[:, lanes].astype(F32)
            near = near_ref[span, lanes]
            far = far_ref[span, lanes]
            full_ref[plane, t, rows : rows + HALO, :] = jnp.where(is_even, near, far)
            full_ref[plane, t, rows + HALO : total, :] = jnp.where(is_even, far, near)
    for k in range(points):
        cosine = trig_ref[k, 0, 0][0:1, :]
        sine = trig_ref[k, 0, 1][0:1, :]
        low = row < HALO
        edge = jnp.where(low, last.astype(F32), first.astype(F32))
        co = jnp.where(edge > 0.5, cosine, 1.0)
        si = jnp.where(edge > 0.5, jnp.where(low, sine, -sine), 0.0)
        for t in range(tiles):
            re = full_ref[2 * k, t, rows:total, :]
            im = full_ref[2 * k + 1, t, rows:total, :]
            full_ref[2 * k, t, rows:total, :] = re * co - im * si
            full_ref[2 * k + 1, t, rows:total, :] = re * si + im * co
    y_even = even("gy")
    lane = lax.broadcasted_iota(jnp.int32, (total, LANES), 1)
    near_acc = jnp.zeros((total, LANES), F32)
    far_acc = jnp.zeros((total, LANES), F32)
    for plane in range(planes):
        left = full_ref[plane, 0]
        right = full_ref[plane, tiles - 1]
        base = plane * SLOT
        keep = (lane >= base) & (lane < base + HALO)
        to_left = jnp.int32(base)
        to_right = jnp.int32((base + HALO) % LANES)
        near = pltpu.roll(jnp.where(y_even, right, left), jnp.where(y_even, to_right, to_left), 1)
        far = pltpu.roll(jnp.where(y_even, left, right), jnp.where(y_even, to_left, to_right), 1)
        near_acc = jnp.where(keep, near, near_acc)
        far_acc = jnp.where(keep, far, far_acc)
    near_out[...] = near_acc
    far_out[...] = far_acc


def solve(full_ref, near_ref, far_ref, table_ref, trig_ref, out_ref, gram_ref,
          halo_ref, cell_ref, b_ref, x_ref, keep_ref):
    planes, tiles, total, _ = full_ref.shape
    points = planes // 2
    rows = out_ref.shape[4]
    mats = table_ref.shape[1]
    count = total // SUB
    y_even = even("gy")
    first = lax.axis_index("gy") == 0
    last = lax.axis_index("gy") == lax.axis_size("gy") - 1

    lane = lax.broadcasted_iota(jnp.int32, (total, LANES), 1)
    right_src = jnp.where(y_even, near_ref[...], far_ref[...])
    left_src = jnp.where(y_even, far_ref[...], near_ref[...])
    is_right = lane < HALO
    is_left = lane >= LANES - HALO
    for plane in range(planes):
        right = pltpu.roll(right_src, (LANES - plane * SLOT) % LANES, 1)
        left = pltpu.roll(left_src, (LANES - HALO - plane * SLOT) % LANES, 1)
        halo_ref[plane] = jnp.where(is_right, right, jnp.where(is_left, left, 0.0))
    edge = jnp.where(is_right, last.astype(F32), jnp.where(is_left, first.astype(F32), 0.0))
    for k in range(points):
        cosine = trig_ref[k, 1, 0][0:1, :]
        sine = trig_ref[k, 1, 1][0:1, :]
        co = jnp.where(edge > 0.5, cosine, 1.0)
        si = jnp.where(edge > 0.5, jnp.where(is_right, sine, -sine), 0.0)
        re = halo_ref[2 * k]
        im = halo_ref[2 * k + 1]
        halo_ref[2 * k] = re * co - im * si
        halo_ref[2 * k + 1] = re * si + im * co

    def rows_of(plane, t, v):
        span = pl.ds(v, SUB, stride=count)
        if t < tiles:
            return full_ref[plane, t, span, :]
        return halo_ref[plane, span, :]

    for t in range(tiles + 1):
        for v in range(count):
            label = rows_of(planes - 1, t, v)
            picks = [label == float(m) for m in range(1, mats)]

            def pick(e):
                value = table_ref[e, 0]
                for m in range(1, mats):
                    value = jnp.where(picks[m - 1], table_ref[e, m], value)
                return value

            for e in (0, 1):
                cell_ref[e, t, v] = pick(e)
            for e in (4, 5, 6, 7):
                cell_ref[e - 2, t, v] = pick(e)
            weight = (pick(2), pick(3))
            for k in range(points):
                z = (rows_of(2 * k, t, v), rows_of(2 * k + 1, t, v))
                for c, value in enumerate(cmul(weight, z)):
                    b_ref[k, c, t, v] = value
                    x_ref[0, k, c, t, v] = value

    lane8 = lax.broadcasted_iota(jnp.int32, (SUB, LANES), 1)
    at_first = lane8 == 0
    at_last = lane8 == LANES - 1

    def sweep(i, carry):
        src = lax.rem(i, 2)
        dst = 1 - src
        for k in range(points):
            for v in range(count):
                sides = []
                for c in range(2):
                    mine = [x_ref[src, k, c, t, v] for t in range(tiles + 1)]
                    ahead = [pltpu.roll(value, 1, 1) for value in mine]
                    behind = [pltpu.roll(value, LANES - 1, 1) for value in mine]
                    side = []
                    for t in range(tiles + 1):
                        one = jnp.where(at_first, ahead[t - 1], ahead[t])
                        two = jnp.where(at_last, behind[(t + 1) % (tiles + 1)], behind[t])
                        side.append(one + two)
                    sides.append(side)
                for t in range(tiles + 1):
                    n = []
                    for c in range(2):
                        if v > 0:
                            up = x_ref[src, k, c, t, v - 1]
                        else:
                            up = pltpu.roll(x_ref[src, k, c, t, count - 1], 1, 0)
                        if v < count - 1:
                            down = x_ref[src, k, c, t, v + 1]
                        else:
                            down = pltpu.roll(x_ref[src, k, c, t, 0], SUB - 1, 0)
                        n.append(sides[c][t] + (up + down))
                    inverse = (cell_ref[0, t, v], cell_ref[1, t, v])
                    n = cmul(inverse, n)
                    for c in range(2):
                        x_ref[dst, k, c, t, v] = b_ref[k, c, t, v] + n[c]
        return carry

    for s in range(STEPS):
        lax.fori_loop(0, SWEEPS, sweep, 0)
        final = SWEEPS % 2
        for k in range(points):
            for t in range(tiles + 1):
                for v in range(count):
                    y = (x_ref[final, k, 0, t, v], x_ref[final, k, 1, t, v])
                    if t < tiles:
                        for c in range(2):
                            out_ref[s, k, c, t, pl.ds(v, SUB, stride=count), :] = y[c]
                    if s < STEPS - 1:
                        b = cmul((cell_ref[2, t, v], cell_ref[3, t, v]), y)
                        if s == 0:
                            keep = cmul((cell_ref[4, t, v], cell_ref[5, t, v]), y)
                            for c in range(2):
                                keep_ref[k, c, t, v] = keep[c]
                        else:
                            b = cadd(b, (keep_ref[k, 0, t, v], keep_ref[k, 1, t, v]))
                        for c in range(2):
                            b_ref[k, c, t, v] = b[c]
                            x_ref[0, k, c, t, v] = b[c]

    rows = total - 2 * HALO
    names = STEPS + 1
    zero = jnp.zeros((SUB, LANES), F32)
    line = jnp.zeros((1, LANES), F32)
    lane1 = lax.broadcasted_iota(jnp.int32, (1, LANES), 1)
    entries = [(i, j) for i in range(names) for j in range(i, names)]
    for k in range(points):

        def gather(r, accs):
            accs = list(accs)
            span = pl.ds(pl.multiple_of(r * SUB, SUB), SUB)
            for t in range(tiles):
                fields = [(full_ref[2 * k, t, span, :], full_ref[2 * k + 1, t, span, :])]
                for s in range(STEPS):
                    fields.append((out_ref[s, k, 0, t, span, :], out_ref[s, k, 1, t, span, :]))
                at = 0
                for i, j in entries:
                    if i == j:
                        a = fields[i]
                        accs[at] = accs[at] + (a[0] * a[0] + a[1] * a[1])
                        at += 1
                    else:
                        product = conj_mul(fields[i], fields[j])
                        accs[at] = accs[at] + product[0]
                        accs[at + 1] = accs[at + 1] + product[1]
                        at += 2
            return tuple(accs)

        accs = lax.fori_loop(0, rows // SUB, gather, (zero,) * (names * names))
        for e, acc in enumerate(accs):
            value = jnp.sum(jnp.sum(acc, axis=0, keepdims=True), axis=1, keepdims=True)
            line = jnp.where(lane1 == k * names * names + e, value, line)
    gram_ref[...] = jnp.broadcast_to(line[None], gram_ref.shape)


def finish(full_ref, out_ref, part_ref, chain_ref, size_ref, basis_ref, hess_ref, done_ref, sem):
    planes, tiles, total, _ = full_ref.shape
    points = planes // 2
    rows = total - 2 * HALO
    names = STEPS + 1
    shape = (SUB, LANES)
    line = jnp.sum(part_ref[:, 0, :], axis=0, keepdims=True)
    uppers = []
    inverses = []
    copies = []
    for k in range(points):
        base = k * names * names
        gram = {}
        at = base
        for i in range(names):
            for j in range(i, names):
                width = 1 if i == j else 2
                gram[i, j] = tuple(
                    jnp.broadcast_to(line[:, at + c : at + c + 1], shape) for c in range(width)
                )
                at += width
        upper = {}
        inv = []
        for i in range(names):
            pivot = gram[i, i][0]
            for l in range(i):
                pivot = pivot - (upper[l, i][0] * upper[l, i][0] + upper[l, i][1] * upper[l, i][1])
            root = jnp.sqrt(pivot)
            upper[i, i] = root
            inv.append(1.0 / root)
            for j in range(i + 1, names):
                value = gram[i, j]
                for l in range(i):
                    value = csub(value, conj_mul(upper[l, i], upper[l, j]))
                upper[i, j] = (value[0] * inv[i], value[1] * inv[i])
        uppers.append(upper)
        inverses.append(inv)

        def combine(r, carry):
            span = pl.ds(pl.multiple_of(r * SUB, SUB), SUB)
            for t in range(tiles):
                lanes = slice(t * LANES, (t + 1) * LANES)
                fields = [(full_ref[2 * k, t, span, :], full_ref[2 * k + 1, t, span, :])]
                for s in range(STEPS):
                    fields.append((out_ref[s, k, 0, t, span, :], out_ref[s, k, 1, t, span, :]))
                found = []
                for i in range(names):
                    value = fields[i]
                    for l in range(i):
                        value = csub(value, cmul(upper[l, i], found[l]))
                    value = (value[0] * inv[i], value[1] * inv[i])
                    found.append(value)
                    if i > 0:
                        done_ref[k, i - 1, 0, span, lanes] = value[0]
                        done_ref[k, i - 1, 1, span, lanes] = value[1]
            return carry

        lax.fori_loop(0, rows // SUB, combine, 0)
        copy = pltpu.make_async_copy(done_ref.at[k], basis_ref.at[k], sem.at[k])
        copy.start()
        copies.append(copy)

    lane = lax.broadcasted_iota(jnp.int32, shape, 1)

    def mixed(pick):
        value = pick(0)
        for k in range(1, points):
            value = jnp.where(lane == k, pick(k), value)
        return value

    gamma = size_ref[...]
    inv0 = mixed(lambda k: inverses[k][0])
    column = []
    for j in range(1, names):
        entry = []
        for i in range(j):
            entry.append(tuple(mixed(lambda k: uppers[k][i, j][c]) * inv0 for c in range(2)))
        entry.append((mixed(lambda k: uppers[k][j, j]) * inv0, jnp.zeros(shape, F32)))
        column.append(entry)

    depth = chain_ref.shape[2]
    row = lax.broadcasted_iota(jnp.int32, (depth, LANES), 0)
    tall = lambda value: jnp.broadcast_to(value[0:1], (depth, LANES))
    nil = jnp.zeros((depth, LANES), F32)
    at_top = row == 0
    basis_u = [[(jnp.where(at_top, 1.0, 0.0), nil)]]
    hess = {}
    coords = []
    mus = []
    for k in range(STEPS):
        active = k + 1
        if k == 0:
            found = column[0]
        elif k == 1:
            found = []
            for i in range(3):
                value = (column[1][i][0] * gamma, column[1][i][1] * gamma)
                if i < 2:
                    value = csub(value, cmul(hess[0, 0], coords[0][i]))
                found.append((value[0] / mus[0], value[1] / mus[0]))
        else:
            found = []
            scale = gamma / mus[0]
            for i in range(4):
                value = (column[2][i][0] * gamma, column[2][i][1] * gamma)
                if i < 3:
                    value = csub(value, cmul(hess[0, 0], column[1][i]))
                value = (value[0] * scale, value[1] * scale)
                if i < 2:
                    value = csub(value, cmul(hess[0, 1], coords[0][i]))
                if i < 3:
                    value = csub(value, cmul(hess[1, 1], coords[1][i]))
                found.append((value[0] / mus[1], value[1] / mus[1]))
        coords.append(found)
        current = basis_u[k]
        x = []
        for i in range(active + 1):
            old = current[i] if i < len(current) else (nil, nil)
            value = tuple(jnp.where(at_top, tall(found[i][c]), old[c]) for c in range(2))
            for s in range(chain_ref.shape[0]):
                step = (chain_ref[s, 0], chain_ref[s, 1])
                moved = tuple(pltpu.roll(value[c], 1 << s, 0) for c in range(2))
                value = cadd(value, cmul(step, moved))
            x.append(value)
        total_t = [None] * active
        for turn in range(2):
            inner = []
            for j in range(active):
                acc = (nil, nil)
                for i in range(len(basis_u[j])):
                    acc = cadd(acc, conj_mul(basis_u[j][i], x[i]))
                inner.append(tuple(jnp.sum(acc[c], axis=0, keepdims=True) for c in range(2)))
            for j in range(active):
                for i in range(len(basis_u[j])):
                    x[i] = csub(x[i], cmul(inner[j], basis_u[j][i]))
                total_t[j] = inner[j] if turn == 0 else cadd(total_t[j], inner[j])
        square = nil
        for value in x:
            square = square + (value[0] * value[0] + value[1] * value[1])
        mu = jnp.sqrt(jnp.sum(square, axis=0, keepdims=True))
        mus.append(jnp.broadcast_to(mu, shape))
        basis_u.append([(value[0] / mu, value[1] / mu) for value in x])
        for j in range(active):
            hess[j, k] = tuple(jnp.broadcast_to(total_t[j][c], shape) for c in range(2))
    small_row = lax.broadcasted_iota(jnp.int32, (names, STEPS), 0)
    small_col = lax.broadcasted_iota(jnp.int32, (names, STEPS), 1)
    for p in range(points):
        for c in range(2):
            value = jnp.zeros((names, STEPS), F32)
            for k in range(STEPS):
                for j in range(k + 2):
                    if j <= k:
                        entry = hess[j, k][c]
                    elif c == 0:
                        entry = mus[k]
                    else:
                        continue
                    here = (small_row == j) & (small_col == k)
                    value = jnp.where(here, entry[0:1, p : p + 1], value)
            hess_ref[p, c] = value
    for copy in copies:
        copy.wait()


def call(body, outs, specs, out_specs, scratch=(), limit=16):
    return pl.pallas_call(
        body,
        out_shape=outs,
        in_specs=specs,
        out_specs=out_specs,
        scratch_shapes=list(scratch),
        compiler_params=pltpu.CompilerParams(vmem_limit_bytes=limit * MIB),
    )


def per_device(
    initial_guess_field,
    medium_label,
    principal_entry_addend,
    linearized_block_weight,
    sample_abscissae,
    singularity_locations,
    basis_normalizers,
    spectral_target,
    quasi_periodic_phase,
):
    points, _, rows, columns = initial_guess_field.shape
    blocks, mats, _ = linearized_block_weight.shape
    tiles = columns // LANES
    planes = 2 * points + 1
    total = rows + 2 * HALO
    count = total // SUB
    names = STEPS + 1
    depth = -(-blocks // SUB) * SUB
    levels = (blocks - 1).bit_length()
    devices = lax.axis_size("gx") * lax.axis_size("gy")
    sds = lambda *shape: jax.ShapeDtypeStruct(shape, F32)

    packed = -(-planes * HALO // SUB) * SUB
    near, far = call(
        pack_rows, [sds(packed, columns)] * 2, [VMEM] * 2, [VMEM] * 2, limit=4
    )(initial_guess_field, medium_label)
    far = lax.ppermute(far, "gx", swap_far("gx"))
    near = lax.ppermute(near, "gx", swap_near("gx"))

    table, trig, chain, size = call(
        params,
        [
            sds(8, mats, SUB, LANES),
            sds(points, 2, 2, SUB, LANES),
            sds(levels, 2, depth, LANES),
            sds(SUB, LANES),
        ],
        [SMEM, VMEM, SMEM, SMEM, SMEM, SMEM, SMEM],
        [VMEM] * 4,
        limit=4,
    )(
        principal_entry_addend,
        linearized_block_weight,
        sample_abscissae,
        singularity_locations,
        basis_normalizers,
        spectral_target,
        quasi_periodic_phase,
    )

    full, near, far = call(
        pack_columns,
        [sds(planes, tiles, total, LANES), sds(total, LANES), sds(total, LANES)],
        [VMEM] * 5,
        [VMEM] * 3,
        limit=8,
    )(initial_guess_field, medium_label, near, far, trig)
    far = lax.ppermute(far, "gy", swap_far("gy"))
    near = lax.ppermute(near, "gy", swap_near("gy"))

    wide = (tiles + 1, count, SUB, LANES)
    out, gram = call(
        solve,
        [sds(STEPS, points, 2, tiles, total, LANES), sds(devices, 1, LANES)],
        [VMEM] * 5,
        [VMEM] * 2,
        [
            pltpu.VMEM((planes, total, LANES), F32),
            pltpu.VMEM((6,) + wide, F32),
            pltpu.VMEM((points, 2) + wide, F32),
            pltpu.VMEM((2, points, 2) + wide, F32),
            pltpu.VMEM((points, 2) + wide, F32),
        ],
        limit=32,
    )(full, near, far, table, trig)

    part = lax.all_to_all(gram, ("gx", "gy"), 0, 0, tiled=True)

    basis, hess = call(
        finish,
        [sds(points, STEPS, 2, rows, columns), sds(points, 2, names, STEPS)],
        [VMEM] * 5,
        [ANY, VMEM],
        [
            pltpu.VMEM((points, STEPS, 2, rows, columns), F32),
            pltpu.SemaphoreType.DMA((points,)),
        ],
        limit=16,
    )(full, out, part, chain, size)
    return basis, hess


def solution(mesh):
    return jax.shard_map(
        per_device,
        mesh=mesh,
        in_specs=(P(None, None, "gx", "gy"), P("gx", "gy"), P(), P(), P(), P(), P(), P(), P()),
        out_specs=(P(None, None, None, "gx", "gy"), P()),
        check_vma=False,
    )
```

time: 712 us -> 43.4 us (0.06); the launches traced: 702 us -> 43 us
  other arithmetic: 231 us -> 0 us
  blocking collectives: 159 us -> 9.83 us
  local copies, waits for them, and re-layouts: 103 us -> 9.64 us
  matrix products: 80.5 us -> 0 us
  starting transfers between devices: 81.1 us -> 8.3 us
  waiting for transfers between devices: 43.5 us -> 1.92 us
  Pallas kernels: 0 us -> 12.6 us
    psum x4 -> x0, blocking collectives: 159 us -> none  [the longest x3 117 us: per_device(): lax.psum((part_real, part_imag, part_square), ('gx', 'gy'))]
    add x38 -> x0, other arithmetic: 159 us -> none  [the longest x12 65.8 us: rotate(): imag_part = padded[:, 0] * sine_part + padded[:, 1] * cosine]
    dot_general x67 -> x0, matrix products: 80.5 us -> none  [the longest x2 10.3 us: grid_inner(): jnp.einsum('kcxy,kxy->kc', vectors_now[:, :, 1], grid_field[:, 0], precis...]
    ppermute x48 -> x4, starting transfers between devices: 81.1 us -> 8.3 us  [the longest x1 3.57 us: per_device(): far = lax.ppermute(far, 'gx', swap_far('gx'))]
    squeeze x103 -> x0, local copies, waits for them, and re-layouts: 66.7 us -> none  [the longest x48 33.2 us: block_chain(): current_full[:, block_id + 1, 0]]
    ppermute x48 -> x4, waiting for transfers between devices: 43.5 us -> 1.92 us  [the longest x1 1.91 us: per_device(): far = lax.ppermute(far, 'gy', swap_far('gy'))]
    sub x24 -> x0, other arithmetic: 34.2 us -> none  [the longest x1 29.7 us: block_chain(): multiplier_inphase[block_id] * previous[:, 0]]
    pallas_call x0 -> x5, Pallas kernels: none -> 12.6 us  [the longest x1 8.71 us: per_device(): call(solve, [sds(STEPS, points, 2, tiles, total, LANES), sds(devices, 1,...]
  transfers between devices with their start and end apart: 48 -> 4, of which waited for: 32 -> 1; matrix products, arithmetic and copies ran while one was open for 11% -> 7% of each run, Pallas kernels for 0% -> 3%
where the time goes in v1:
time: 43.4 us; the launch traced here: 43 us
  Pallas kernels  12.6 us (29%)
  blocking collectives  9.83 us (23%)
  local copies, waits for them, and re-layouts  9.64 us (22%)
  starting transfers between devices  8.3 us (19%)
  waiting for transfers between devices  1.92 us (4%)
  between operations  0.72 us (2%)
    all_to_all x1, blocking collectives, per_device(): part = lax.all_to_all(gram, ('gx', 'gy'), 0, 0, tiled=True)  9.83 us
    unnamed x18, local copies, waits for them, and re-layouts  8.94 us
    pallas_call x1, Pallas kernels, per_device(): call(solve, [sds(STEPS, points, 2, tiles, total, LANES), sds(devices, 1,...  8.71 us
    ppermute x1, starting transfers between devices, per_device(): far = lax.ppermute(far, 'gx', swap_far('gx'))  3.57 us
    ppermute x1, starting transfers between devices, per_device(): near = lax.ppermute(near, 'gx', swap_near('gx'))  3.03 us
    pallas_call x1, Pallas kernels, per_device(): call(finish, [sds(points, STEPS, 2, rows, columns), sds(points, 2, names,...  2.26 us
    ppermute x1, waiting for transfers between devices, per_device(): far = lax.ppermute(far, 'gy', swap_far('gy'))  1.91 us
    ppermute x1, starting transfers between devices, per_device(): far = lax.ppermute(far, 'gy', swap_far('gy'))  1.62 us
  transfers between devices with their start and end apart: 4, of which 1 were waited for; matrix products, arithmetic and copies ran while one was open for 7% of the time, Pallas kernels for 3%

profile of v1, /device:TPU:0, one launch (start us, length us, event | category | flops | bytes accessed | tf_op | source)
XLA Modules:
  0.0 43.0 jit_solution(8013028120315055138)
XLA Ops:
  0.6 0.0 copy-start
  0.6 1.0 %copy-done = f32[2,2,64,512]{3,2,1,0:T(8,128)S(1)} copy-done((f32[2,2,64,512]{3,2,1,0:T(8,128)S(1)}, f32[2,2,64,512]{3,2,1,0:T(8,128)}, u32[]{:S(2)}) %copy-start) | copy-done | bytes 524312
  1.7 0.9 %copy-done.2 = s32[64,512]{1,0:T(8,128)S(1)} copy-done((s32[64,512]{1,0:T(8,128)S(1)}, s32[64,512]{1,0:T(8,128)}, u32[]{:S(2)}) %copy-start.2) | copy-done | bytes 131096
  2.6 0.1 shard_map.104
  2.6 3.0 %collective-permute-start = (f32[64,512]{1,0:T(8,128)S(1)}, f32[64,512]{1,0:T(8,128)S(1)}, u32[]{:S(2)}, u32[]{:S(2)}) collective-permute-start(f32[64,512]{1,0:T(8,128)S(1)} %get-tuple-element.13), channel_id=1, source_target_pairs={{0,4},{4,0},{8,12},{12,8},{16,20},{20,16},{24,28},{28,24},{1,5},{5... | collective-permute-start | bytes 393224 | tf_op jit(solution)/shard_map/ppermute | solution.py:558
  5.7 3.6 %collective-permute-start.1 = (f32[64,512]{1,0:T(8,128)S(1)}, f32[64,512]{1,0:T(8,128)S(1)}, u32[]{:S(2)}, u32[]{:S(2)}) collective-permute-start(f32[64,512]{1,0:T(8,128)S(1)} %get-tuple-element.14), channel_id=1, source_target_pairs={{0,28},{4,8},{8,4},{12,16},{16,12},{20,24},{24,20},{28,0},{1,29},{... | collective-permute-start | bytes 393224 | tf_op jit(solution)/shard_map/ppermute | solution.py:557
  9.2 0.8 %copy.11.a_ref = f32[4,2]{1,0:T(4,128)S(1)} copy(f32[4,2]{0,1:T(2,128)} %param.11) | data formatting | bytes 64 | tf_op args[2]
  10.0 0.8 %copy.13.node_ref = f32[24,2]{1,0:T(8,128)S(1)} copy(f32[24,2]{0,1:T(2,128)} %param.13) | data formatting | bytes 384 | tf_op args[4]
  10.8 0.8 %copy.14.pole_ref = f32[24,2]{1,0:T(8,128)S(1)} copy(f32[24,2]{0,1:T(2,128)} %param.14) | data formatting | bytes 384 | tf_op args[5]
  11.5 0.8 %copy.12.w_ref = f32[25,4,2]{2,1,0:T(4,128)S(1)} copy(f32[25,4,2]{0,2,1:T(2,128)} %param.12) | data formatting | bytes 1600 | tf_op args[3]
  12.3 0.7 %copy-done.4 = f32[2,2]{1,0:T(2,128)S(1)} copy-done((f32[2,2]{1,0:T(2,128)S(1)}, f32[2,2]{1,0:T(2,128)}, u32[]{:S(2)}) %copy-start.4) | copy-done | bytes 40
  13.0 0.7 %copy-done.5 = f32[24]{0:T(128)S(1)} copy-done((f32[24]{0:T(128)S(1)}, f32[24]{0:T(128)}, u32[]{:S(2)}) %copy-start.5) | copy-done | bytes 120
  13.7 0.7 %copy-done.6 = f32[2]{0:T(128)S(1)} copy-done((f32[2]{0:T(128)S(1)}, f32[2]{0:T(128)}, u32[]{:S(2)}) %copy-start.6) | copy-done | bytes 32
  14.3 1.3 %shard_map.105 = (f32[8,4,8,128]{3,2,1,0:T(8,128)S(1)}, f32[2,2,2,8,128]{4,3,2,1,0:T(8,128)S(1)}, f32[5,2,32,128]{3,2,1,0:T(8,128)S(1)}, f32[8,128]{1,0:T(8,128)S(1)}) custom-call(f32[4,2]{1,0:T(4,128)S(1)} %copy.11.a_ref, f32[25,4,2]{2,1,0:T(4,128)S(1)} %copy.12.w_ref, f32[24,2]{1,0:T(8,128)S(1)} %copy.13.node_ref, f32[24,2]{1,0:T(8,128)S(1)} %copy.14.pole_ref, ...), custom_call_target="tpu_custom_call" | custom-call | tf_op jit(solution)/shard_map/pallas_call | solution.py:560
  15.7 1.0 %copy-done.1 = f32[2,2,64,512]{3,2,1,0:T(8,128)S(1)} copy-done((f32[2,2,64,512]{3,2,1,0:T(8,128)S(1)}, f32[2,2,64,512]{3,2,1,0:T(8,128)}, u32[]{:S(2)}) %copy-start.1) | copy-done | bytes 524312
  16.7 0.9 %copy-done.3 = s32[64,512]{1,0:T(8,128)S(1)} copy-done((s32[64,512]{1,0:T(8,128)S(1)}, s32[64,512]{1,0:T(8,128)}, u32[]{:S(2)}) %copy-start.3) | copy-done | bytes 131096
  17.6 0.2 shard_map.106
  17.9 0.1 collective-permute-start.2
  17.9 1.6 %collective-permute-start.3 = (f32[88,128]{1,0:T(8,128)S(1)}, f32[88,128]{1,0:T(8,128)S(1)}, u32[]{:S(2)}, u32[]{:S(2)}) collective-permute-start(f32[88,128]{1,0:T(8,128)S(1)} %get-tuple-element.18), channel_id=1, source_target_pairs={{0,3},{1,2},{2,1},{3,0},{4,7},{5,6},{6,5},{7,4},{8,11},{9,10},{10,... | collective-permute-start | bytes 135176 | tf_op jit(solution)/shard_map/ppermute | solution.py:588
  19.6 1.9 %collective-permute-done.3.far_ref = f32[88,128]{1,0:T(8,128)S(1)} collective-permute-done((f32[88,128]{1,0:T(8,128)S(1)}, f32[88,128]{1,0:T(8,128)S(1)}, u32[]{:S(2)}, u32[]{:S(2)}) %collective-permute-start.3) | collective-permute-done | bytes 45088 | tf_op jit(solution)/shard_map/ppermute | solution.py:588
  21.5 8.7 %shard_map.107 = (f32[3,2,2,4,88,128]{5,4,3,2,1,0:T(8,128)S(1)}, f32[32,1,128]{2,1,0:T(1,128)S(1)}) custom-call(f32[5,4,88,128]{3,2,1,0:T(8,128)S(1)} %get-tuple-element.16.full_ref, f32[88,128]{1,0:T(8,128)S(1)} %collective-permute-done.2.near_ref, f32[88,128]{1,0:T(8,128)S(1)} %collective-permute-done.3.far_ref, ...), custom_call_target="tpu_custom_call" | custom-call | tf_op jit(solution)/shard_map/pallas_call | solution.py:592
  30.2 9.8 %all_to_all.5.part_ref = f32[32,1,128]{2,1,0:T(1,128)S(1)} all-to-all(f32[32,1,128]{2,1,0:T(1,128)S(1)} %get-tuple-element.21), channel_id=1, replica_groups=mesh['gx'=8,'gy'=4] {'gx','gy'}, dimensions={0} | all-to-all | bytes 32768 | tf_op jit(solution)/shard_map/all_to_all | solution.py:607
  40.0 2.3 %shard_map.108 = (f32[2,3,2,64,512]{4,3,2,1,0:T(8,128)}, f32[2,2,4,3]{3,2,1,0:T(4,128)S(1)}) custom-call(f32[5,4,88,128]{3,2,1,0:T(8,128)S(1)} %get-tuple-element.16.full_ref, f32[3,2,2,4,88,128]{5,4,3,2,1,0:T(8,128)S(1)} %get-tuple-element.20.out_ref, f32[32,1,128]{2,1,0:T(1,128)S(1)} %all_to_all.5.part_ref, ...), custom_call_target="tpu_custom_call" | custom-call | tf_op jit(solution)/shard_map/pallas_call | solution.py:609
  42.3 0.7 %copy.15 = f32[2,2,4,3]{2,1,3,0:T(2,128)} copy(f32[2,2,4,3]{3,2,1,0:T(4,128)S(1)} %get-tuple-element.25) | data formatting | bytes 384 | tf_op jit(solution)/shard_map/pallas_call | solution.py:609
  (9 shorter events, 0.0 us)
Async XLA Ops:
  0.6 1.0 %copy-start = (f32[2,2,64,512]{3,2,1,0:T(8,128)S(1)}, f32[2,2,64,512]{3,2,1,0:T(8,128)}, u32[]{:S(2)}) copy-start(f32[2,2,64,512]{3,2,1,0:T(8,128)} %z_ref.3) | copy-start | bytes 1572868
  1.7 0.9 %copy-start.2 = (s32[64,512]{1,0:T(8,128)S(1)}, s32[64,512]{1,0:T(8,128)}, u32[]{:S(2)}) copy-start(s32[64,512]{1,0:T(8,128)} %m_ref.3) | copy-start | bytes 393220
  2.6 13.0 %collective-permute-start = (f32[64,512]{1,0:T(8,128)S(1)}, f32[64,512]{1,0:T(8,128)S(1)}, u32[]{:S(2)}, u32[]{:S(2)}) collective-permute-start(f32[64,512]{1,0:T(8,128)S(1)} %get-tuple-element.13), channel_id=1, source_target_pairs={{0,4},{4,0},{8,12},{12,8},{16,20},{20,16},{24,28},{28,24},{1,5},{5... | collective-permute-start | bytes 393224 | tf_op jit(solution)/shard_map/ppermute | solution.py:558
  5.7 10.0 %collective-permute-start.1 = (f32[64,512]{1,0:T(8,128)S(1)}, f32[64,512]{1,0:T(8,128)S(1)}, u32[]{:S(2)}, u32[]{:S(2)}) collective-permute-start(f32[64,512]{1,0:T(8,128)S(1)} %get-tuple-element.14), channel_id=1, source_target_pairs={{0,28},{4,8},{8,4},{12,16},{16,12},{20,24},{24,20},{28,0},{1,29},{... | collective-permute-start | bytes 393224 | tf_op jit(solution)/shard_map/ppermute | solution.py:557
  12.3 0.7 %copy-start.4 = (f32[2,2]{1,0:T(2,128)S(1)}, f32[2,2]{1,0:T(2,128)}, u32[]{:S(2)}) copy-start(f32[2,2]{1,0:T(2,128)} %phase_ref.1) | copy-start | bytes 52
  13.0 0.7 %copy-start.5 = (f32[24]{0:T(128)S(1)}, f32[24]{0:T(128)}, u32[]{:S(2)}) copy-start(f32[24]{0:T(128)} %scale_ref.1) | copy-start | bytes 292
  13.7 0.7 %copy-start.6 = (f32[2]{0:T(128)S(1)}, f32[2]{0:T(128)}, u32[]{:S(2)}) copy-start(f32[2]{0:T(128)} %target_ref.1) | copy-start | bytes 28
  15.7 1.0 %copy-start.1 = (f32[2,2,64,512]{3,2,1,0:T(8,128)S(1)}, f32[2,2,64,512]{3,2,1,0:T(8,128)}, u32[]{:S(2)}) copy-start(f32[2,2,64,512]{3,2,1,0:T(8,128)} %z_ref.3) | copy-start | bytes 1572868
  16.7 0.9 %copy-start.3 = (s32[64,512]{1,0:T(8,128)S(1)}, s32[64,512]{1,0:T(8,128)}, u32[]{:S(2)}) copy-start(s32[64,512]{1,0:T(8,128)} %m_ref.3) | copy-start | bytes 393220
  17.9 1.7 %collective-permute-start.2 = (f32[88,128]{1,0:T(8,128)S(1)}, f32[88,128]{1,0:T(8,128)S(1)}, u32[]{:S(2)}, u32[]{:S(2)}) collective-permute-start(f32[88,128]{1,0:T(8,128)S(1)} %get-tuple-element.17), channel_id=1, source_target_pairs={{0,1},{1,0},{2,3},{3,2},{4,5},{5,4},{6,7},{7,6},{8,9},{9,8},{10,11... | collective-permute-start | bytes 135176 | tf_op jit(solution)/shard_map/ppermute | solution.py:589
  17.9 3.5 %collective-permute-start.3 = (f32[88,128]{1,0:T(8,128)S(1)}, f32[88,128]{1,0:T(8,128)S(1)}, u32[]{:S(2)}, u32[]{:S(2)}) collective-permute-start(f32[88,128]{1,0:T(8,128)S(1)} %get-tuple-element.18), channel_id=1, source_target_pairs={{0,3},{1,2},{2,1},{3,0},{4,7},{5,6},{6,5},{7,4},{8,11},{9,10},{10,... | collective-permute-start | bytes 135176 | tf_op jit(solution)/shard_map/ppermute | solution.py:588

commit v2 on v1

--- a/solution.py
+++ b/solution.py
@@ -1,11 +1,10 @@
-import functools
-
 import jax
 import jax.numpy as jnp
 from jax import lax
 from jax.experimental import pallas as pl
 from jax.experimental.pallas import tpu as pltpu
 from jax.sharding import PartitionSpec as P
+
 
 STEPS = 3
 SWEEPS = 4
@@ -17,6 +16,7 @@
 VMEM = pl.BlockSpec(memory_space=pltpu.VMEM)
 SMEM = pl.BlockSpec(memory_space=pltpu.SMEM)
 ANY = pl.BlockSpec(memory_space=pl.ANY)
+HBM = pl.BlockSpec(memory_space=pltpu.HBM)
 MIB = 1024 * 1024
 
 
@@ -49,82 +49,129 @@
     return (a[0] * b[0] + a[1] * b[1], a[0] * b[1] - a[1] * b[0])
 
 
-def pack_rows(z_ref, m_ref, near_ref, far_ref):
-    points, _, rows, _ = z_ref.shape
-    is_even = even("gx")
-    for plane in range(2 * points + 1):
-        if plane < 2 * points:
-            top = z_ref[plane // 2, plane % 2, 0:HALO, :]
-            bottom = z_ref[plane // 2, plane % 2, rows - HALO : rows, :]
-        else:
-            top = m_ref[0:HALO, :].astype(F32)
-            bottom = m_ref[rows - HALO : rows, :].astype(F32)
+def pack_lanes(sides):
+    y_even = even("gy")
+    shape = sides[0][0].shape
+    lane = lax.broadcasted_iota(jnp.int32, shape, 1)
+    near_acc = jnp.zeros(shape, F32)
+    far_acc = jnp.zeros(shape, F32)
+    for plane, (left, right) in enumerate(sides):
+        base = plane * SLOT
+        keep = (lane >= base) & (lane < base + HALO)
+        to_left = jnp.int32(base)
+        to_right = jnp.int32((base + HALO) % LANES)
+        near = pltpu.roll(jnp.where(y_even, right, left), jnp.where(y_even, to_right, to_left), 1)
+        far = pltpu.roll(jnp.where(y_even, left, right), jnp.where(y_even, to_left, to_right), 1)
+        near_acc = jnp.where(keep, near, near_acc)
+        far_acc = jnp.where(keep, far, far_acc)
+    return near_acc, far_acc
+
+
+def pack_corners(near_x, far_x, near_c, far_c, side_ref):
+    planes = side_ref.shape[0]
+    columns = near_x.shape[1]
+    x_even = even("gx")
+    for plane in range(planes):
         span = slice(plane * HALO, (plane + 1) * HALO)
-        near_ref[span, :] = jnp.where(is_even, bottom, top)
-        far_ref[span, :] = jnp.where(is_even, top, bottom)
+        for side, lanes in enumerate((slice(0, LANES), slice(columns - LANES, columns))):
+            near = near_x[span, lanes]
+            far = far_x[span, lanes]
+            side_ref[plane, side, 0:HALO, :] = jnp.where(x_even, near, far)
+            side_ref[plane, side, HALO : 2 * HALO, :] = jnp.where(x_even, far, near)
+    near_c[...], far_c[...] = pack_lanes([(side_ref[p, 0], side_ref[p, 1]) for p in range(planes)])
+
+
+def pack(z_hbm, m_hbm, a_hbm, w_hbm, node_hbm, pole_hbm, scale_hbm, target_hbm, phase_hbm,
+         full_ref, near_x, far_x, near_y, far_y,
+         a_ref, w_ref, node_ref, pole_ref, scale_ref, target_ref, phase_ref, label_ref, sem):
+    points, _, rows, columns = z_hbm.shape
+    tiles = columns // LANES
+    planes = 2 * points + 1
+    pairs = []
+    for t in range(tiles):
+        lanes = pl.ds(t * LANES, LANES)
+        for plane in range(2 * points):
+            src = z_hbm.at[plane // 2, plane % 2, :, lanes]
+            pairs.append((src, full_ref.at[plane, t, pl.ds(0, rows), :]))
+        pairs.append((m_hbm.at[:, lanes], label_ref.at[t]))
+    pairs += [(a_hbm, a_ref), (w_hbm, w_ref), (node_hbm, node_ref), (pole_hbm, pole_ref)]
+    pairs += [(scale_hbm, scale_ref), (target_hbm, target_ref), (phase_hbm, phase_ref)]
+    copies = [pltpu.make_async_copy(src, dst, sem.at[n]) for n, (src, dst) in enumerate(pairs)]
+    for copy in copies:
+        copy.start()
+    for copy in copies:
+        copy.wait()
+    for t in range(tiles):
+        full_ref[planes - 1, t, 0:rows, :] = label_ref[t].astype(F32)
+    x_even = even("gx")
+    sides = [(full_ref[p, 0, 0:rows, :], full_ref[p, tiles - 1, 0:rows, :]) for p in range(planes)]
+    near_acc, far_acc = pack_lanes(sides)
+    near_y[...] = near_acc
+    far_y[...] = far_acc
+    for plane in range(planes):
+        span = slice(plane * HALO, (plane + 1) * HALO)
+        for t in range(tiles):
+            lanes = slice(t * LANES, (t + 1) * LANES)
+            top = full_ref[plane, t, 0:HALO, :]
+            bottom = full_ref[plane, t, rows - HALO : rows, :]
+            near_x[span, lanes] = jnp.where(x_even, bottom, top)
+            far_x[span, lanes] = jnp.where(x_even, top, bottom)
 
 
 def params(a_ref, w_ref, node_ref, pole_ref, scale_ref, target_ref, phase_ref,
            table_ref, trig_ref, chain_ref, size_ref):
     shape = (SUB, LANES)
 
-    def splat(value):
-        return jnp.full(shape, value, F32)
-
-    mats = a_ref.shape[0]
-    totals = node_ref.shape[0]
-    target = (splat(target_ref[0]), splat(target_ref[1]))
-    steps = []
-    for j in range(totals):
-        gap = csub(target, (splat(node_ref[j, 0]), splat(node_ref[j, 1])))
-        pole = (splat(pole_ref[j, 0]), splat(pole_ref[j, 1]))
-        pole_size = pole[0] * pole[0] + pole[1] * pole[1]
-        quotient = conj_mul(pole, target)
-        quotient = (quotient[0] / pole_size, quotient[1] / pole_size)
-        scale = splat(scale_ref[j])
-        lower = (scale * (1.0 - quotient[0]), -scale * quotient[1])
-        size = lower[0] * lower[0] + lower[1] * lower[1]
-        factor = conj_mul(lower, gap)
-        steps.append((factor[0] / size, factor[1] / size))
+    def full(value):
+        return jnp.broadcast_to(value, shape)
+
+    mats = a_ref.shape[1]
+    totals = node_ref.shape[1]
+    target = (target_ref[:, 0:1], target_ref[:, 1:2])
+    gap = csub(target, (node_ref[0:1, :], node_ref[1:2, :]))
+    pole = (pole_ref[0:1, :], pole_ref[1:2, :])
+    pole_size = pole[0] * pole[0] + pole[1] * pole[1]
+    quotient = conj_mul(pole, target)
+    quotient = (quotient[0] / pole_size, quotient[1] / pole_size)
+    scale = scale_ref[...]
+    lower = (scale * (1.0 - quotient[0]), -scale * quotient[1])
+    lower_size = lower[0] * lower[0] + lower[1] * lower[1]
+    factor = conj_mul(lower, gap)
+    factor = (factor[0] / lower_size, factor[1] / lower_size)
+    steps = [tuple(full(factor[c][:, j : j + 1]) for c in range(2)) for j in range(totals)]
     zero = jnp.zeros(shape, F32)
-    power = (splat(1.0), zero)
-    size = splat(1.0)
-    sums = [zero[:mats, :2]] * 4
-    for b in range(totals + 1):
-        if b > 0:
-            power = cmul(power, steps[b - 1])
-            size = size + power[0] * power[0] + power[1] * power[1]
-        w = w_ref[b]
-        pr = power[0][:mats, :2]
-        pi = power[1][:mats, :2]
-        sums[0] = sums[0] + w * pr
-        sums[1] = sums[1] + w * pi
-        sums[2] = sums[2] + float(b) * (w * pr)
-        sums[3] = sums[3] + float(b) * (w * pi)
+    lane = lax.broadcasted_iota(jnp.int32, shape, 1)
+    power = (jnp.ones(shape, F32), zero)
+    size = jnp.ones(shape, F32)
+    powers = [jnp.where(lane == 0, power[0], zero), zero]
+    for b in range(1, totals + 1):
+        power = cmul(power, steps[b - 1])
+        size = size + (power[0] * power[0] + power[1] * power[1])
+        for c in range(2):
+            powers[c] = jnp.where(lane == b, power[c], powers[c])
     gamma = jnp.sqrt(size)
     size_ref[...] = gamma
-
-    def full(value):
-        return jnp.broadcast_to(value, shape)
-
+    blocks = totals + 1
+    line = tuple((powers[c] / gamma)[0:1, :blocks] for c in range(2))
+    order = lax.broadcasted_iota(jnp.int32, (1, blocks), 1).astype(F32)
     for m in range(mats):
-        center = 4.0 + splat(a_ref[m, 0])
-        side = splat(a_ref[m, 1])
-        lower = center * center + side * side
-        inverse = (center / lower, -side / lower)
-        first = (full(w_ref[0, m : m + 1, 0:1]), full(w_ref[0, m : m + 1, 1:2]))
-        parts = [[full(s[m : m + 1, c : c + 1]) for c in range(2)] for s in sums]
-        a_weight = (parts[0][0] - parts[1][1], parts[0][1] + parts[1][0])
-        b_weight = (parts[2][0] - parts[3][1], parts[2][1] + parts[3][0])
-        a_weight = (a_weight[0] / gamma, a_weight[1] / gamma)
-        b_weight = (b_weight[0] / gamma / gamma, b_weight[1] / gamma / gamma)
+        center = 4.0 + full(a_ref[0:1, m : m + 1])
+        side = full(a_ref[1:2, m : m + 1])
+        inverse_size = center * center + side * side
+        inverse = (center / inverse_size, -side / inverse_size)
+        w = (w_ref[m, 0:1, :], w_ref[m, 1:2, :])
+        first = (full(w[0][:, 0:1]), full(w[1][:, 0:1]))
+        product = cmul(w, line)
+        a_weight = tuple(full(jnp.sum(p, axis=1, keepdims=True)) for p in product)
+        b_weight = tuple(full(jnp.sum(p * order, axis=1, keepdims=True)) for p in product)
+        b_weight = (b_weight[0] / gamma, b_weight[1] / gamma)
         entries = (inverse, cmul(inverse, first), cmul(inverse, a_weight), cmul(inverse, b_weight))
         for e, (re, im) in enumerate(entries):
             table_ref[2 * e, m] = re
             table_ref[2 * e + 1, m] = im
     for k in range(phase_ref.shape[0]):
         for axis in range(2):
-            angle = splat(phase_ref[k, axis])
+            angle = full(phase_ref[k : k + 1, axis : axis + 1])
             trig_ref[k, axis, 0] = jnp.cos(angle)
             trig_ref[k, axis, 1] = jnp.sin(angle)
     depth = chain_ref.shape[2]
@@ -146,88 +193,69 @@
         step = cmul(step, moved)
 
 
-def pack_columns(z_ref, m_ref, near_ref, far_ref, trig_ref, full_ref, near_out, far_out):
-    points, _, rows, columns = z_ref.shape
-    tiles = columns // LANES
-    planes = 2 * points + 1
-    total = rows + 2 * HALO
-    is_even = even("gx")
-    first = lax.axis_index("gx") == 0
-    last = lax.axis_index("gx") == lax.axis_size("gx") - 1
-    row = lax.broadcasted_iota(jnp.int32, (2 * HALO, LANES), 0)
+def solve(own_ref, near_x, far_x, near_y, far_y, near_c, far_c,
+          table_ref, trig_ref, out_ref, gram_ref,
+          full_ref, edge_ref, halo_ref, cell_ref, b_ref, x_ref, keep_ref):
+    planes, tiles, total, _ = own_ref.shape
+    points = planes // 2
+    rows = total - 2 * HALO
+    mats = table_ref.shape[1]
+    count = total // SUB
+    x_even = even("gx")
+    y_even = even("gy")
+
     for plane in range(planes):
         span = slice(plane * HALO, (plane + 1) * HALO)
         for t in range(tiles):
             lanes = slice(t * LANES, (t + 1) * LANES)
-            if plane < 2 * points:
-                full_ref[plane, t, 0:rows, :] = z_ref[plane // 2, plane % 2, :, lanes]
-            else:
-                full_ref[plane, t, 0:rows, :] = m_ref[:, lanes].astype(F32)
-            near = near_ref[span, lanes]
-            far = far_ref[span, lanes]
-            full_ref[plane, t, rows : rows + HALO, :] = jnp.where(is_even, near, far)
-            full_ref[plane, t, rows + HALO : total, :] = jnp.where(is_even, far, near)
-    for k in range(points):
-        cosine = trig_ref[k, 0, 0][0:1, :]
-        sine = trig_ref[k, 0, 1][0:1, :]
-        low = row < HALO
-        edge = jnp.where(low, last.astype(F32), first.astype(F32))
-        co = jnp.where(edge > 0.5, cosine, 1.0)
-        si = jnp.where(edge > 0.5, jnp.where(low, sine, -sine), 0.0)
-        for t in range(tiles):
-            re = full_ref[2 * k, t, rows:total, :]
-            im = full_ref[2 * k + 1, t, rows:total, :]
-            full_ref[2 * k, t, rows:total, :] = re * co - im * si
-            full_ref[2 * k + 1, t, rows:total, :] = re * si + im * co
-    y_even = even("gy")
+            near = near_x[span, lanes]
+            far = far_x[span, lanes]
+            full_ref[plane, t, 0:rows, :] = own_ref[plane, t, 0:rows, :]
+            full_ref[plane, t, rows : rows + HALO, :] = jnp.where(x_even, near, far)
+            full_ref[plane, t, rows + HALO : total, :] = jnp.where(x_even, far, near)
+    for side in range(2):
+        keep = y_even if side == 0 else jnp.logical_not(y_even)
+        edge_ref[side, 0:rows, :] = jnp.where(keep, near_y[...], far_y[...])
+        edge_ref[side, rows:total, :] = jnp.where(keep, near_c[...], far_c[...])
+
     lane = lax.broadcasted_iota(jnp.int32, (total, LANES), 1)
-    near_acc = jnp.zeros((total, LANES), F32)
-    far_acc = jnp.zeros((total, LANES), F32)
-    for plane in range(planes):
-        left = full_ref[plane, 0]
-        right = full_ref[plane, tiles - 1]
-        base = plane * SLOT
-        keep = (lane >= base) & (lane < base + HALO)
-        to_left = jnp.int32(base)
-        to_right = jnp.int32((base + HALO) % LANES)
-        near = pltpu.roll(jnp.where(y_even, right, left), jnp.where(y_even, to_right, to_left), 1)
-        far = pltpu.roll(jnp.where(y_even, left, right), jnp.where(y_even, to_left, to_right), 1)
-        near_acc = jnp.where(keep, near, near_acc)
-        far_acc = jnp.where(keep, far, far_acc)
-    near_out[...] = near_acc
-    far_out[...] = far_acc
-
-
-def solve(full_ref, near_ref, far_ref, table_ref, trig_ref, out_ref, gram_ref,
-          halo_ref, cell_ref, b_ref, x_ref, keep_ref):
-    planes, tiles, total, _ = full_ref.shape
-    points = planes // 2
-    rows = out_ref.shape[4]
-    mats = table_ref.shape[1]
-    count = total // SUB
-    y_even = even("gy")
-    first = lax.axis_index("gy") == 0
-    last = lax.axis_index("gy") == lax.axis_size("gy") - 1
-
-    lane = lax.broadcasted_iota(jnp.int32, (total, LANES), 1)
-    right_src = jnp.where(y_even, near_ref[...], far_ref[...])
-    left_src = jnp.where(y_even, far_ref[...], near_ref[...])
     is_right = lane < HALO
     is_left = lane >= LANES - HALO
+    right_src = edge_ref[0]
+    left_src = edge_ref[1]
     for plane in range(planes):
         right = pltpu.roll(right_src, (LANES - plane * SLOT) % LANES, 1)
         left = pltpu.roll(left_src, (LANES - HALO - plane * SLOT) % LANES, 1)
         halo_ref[plane] = jnp.where(is_right, right, jnp.where(is_left, left, 0.0))
-    edge = jnp.where(is_right, last.astype(F32), jnp.where(is_left, first.astype(F32), 0.0))
+
+    def ends(axis):
+        first = (lax.axis_index(axis) == 0).astype(F32)
+        last = (lax.axis_index(axis) == lax.axis_size(axis) - 1).astype(F32)
+        return first, last
+
+    first, last = ends("gx")
+    low = lax.broadcasted_iota(jnp.int32, (2 * HALO, LANES), 0) < HALO
+    x_edge = jnp.where(low, last, first) > 0.5
+    first, last = ends("gy")
+    y_edge = jnp.where(is_right, last, jnp.where(is_left, first, 0.0)) > 0.5
     for k in range(points):
-        cosine = trig_ref[k, 1, 0][0:1, :]
+        sine = trig_ref[k, 0, 1][0:1, :]
+        co = jnp.where(x_edge, trig_ref[k, 0, 0][0:1, :], 1.0)
+        si = jnp.where(x_edge, jnp.where(low, sine, -sine), 0.0)
+        for t in range(tiles + 1):
+            if t < tiles:
+                parts = (full_ref.at[2 * k, t], full_ref.at[2 * k + 1, t])
+            else:
+                parts = (halo_ref.at[2 * k], halo_ref.at[2 * k + 1])
+            turned = cmul((parts[0][rows:total, :], parts[1][rows:total, :]), (co, si))
+            parts[0][rows:total, :] = turned[0]
+            parts[1][rows:total, :] = turned[1]
         sine = trig_ref[k, 1, 1][0:1, :]
-        co = jnp.where(edge > 0.5, cosine, 1.0)
-        si = jnp.where(edge > 0.5, jnp.where(is_right, sine, -sine), 0.0)
-        re = halo_ref[2 * k]
-        im = halo_ref[2 * k + 1]
-        halo_ref[2 * k] = re * co - im * si
-        halo_ref[2 * k + 1] = re * si + im * co
+        co = jnp.where(y_edge, trig_ref[k, 1, 0][0:1, :], 1.0)
+        si = jnp.where(y_edge, jnp.where(is_right, sine, -sine), 0.0)
+        turned = cmul((halo_ref[2 * k], halo_ref[2 * k + 1]), (co, si))
+        halo_ref[2 * k] = turned[0]
+        halo_ref[2 * k + 1] = turned[1]
 
     def rows_of(plane, t, v):
         span = pl.ds(v, SUB, stride=count)
@@ -317,7 +345,6 @@
                             b_ref[k, c, t, v] = b[c]
                             x_ref[0, k, c, t, v] = b[c]
 
-    rows = total - 2 * HALO
     names = STEPS + 1
     zero = jnp.zeros((SUB, LANES), F32)
     line = jnp.zeros((1, LANES), F32)
@@ -496,22 +523,17 @@
         basis_u.append([(value[0] / mu, value[1] / mu) for value in x])
         for j in range(active):
             hess[j, k] = tuple(jnp.broadcast_to(total_t[j][c], shape) for c in range(2))
-    small_row = lax.broadcasted_iota(jnp.int32, (names, STEPS), 0)
-    small_col = lax.broadcasted_iota(jnp.int32, (names, STEPS), 1)
+    part_row = lax.broadcasted_iota(jnp.int32, (2, names), 0)
+    part_lane = lax.broadcasted_iota(jnp.int32, (2, names), 1)
     for p in range(points):
-        for c in range(2):
-            value = jnp.zeros((names, STEPS), F32)
-            for k in range(STEPS):
-                for j in range(k + 2):
-                    if j <= k:
-                        entry = hess[j, k][c]
-                    elif c == 0:
-                        entry = mus[k]
-                    else:
-                        continue
-                    here = (small_row == j) & (small_col == k)
+        for k in range(STEPS):
+            value = jnp.zeros((2, names), F32)
+            for j in range(k + 2):
+                parts = hess[j, k] if j <= k else (mus[k],)
+                for c, entry in enumerate(parts):
+                    here = (part_row == c) & (part_lane == j)
                     value = jnp.where(here, entry[0:1, p : p + 1], value)
-            hess_ref[p, c] = value
+            hess_ref[p, k] = value
     for copy in copies:
         copy.wait()
 
@@ -551,11 +573,38 @@
     sds = lambda *shape: jax.ShapeDtypeStruct(shape, F32)
 
     packed = -(-planes * HALO // SUB) * SUB
-    near, far = call(
-        pack_rows, [sds(packed, columns)] * 2, [VMEM] * 2, [VMEM] * 2, limit=4
-    )(initial_guess_field, medium_label)
-    far = lax.ppermute(far, "gx", swap_far("gx"))
-    near = lax.ppermute(near, "gx", swap_near("gx"))
+    small = [
+        principal_entry_addend.T,
+        linearized_block_weight.transpose(1, 2, 0),
+        sample_abscissae.T,
+        singularity_locations.T,
+        basis_normalizers.reshape(1, -1),
+        spectral_target.reshape(1, -1),
+        quasi_periodic_phase,
+    ]
+    full, *sends = call(
+        pack,
+        [sds(planes, tiles, total, LANES)]
+        + [sds(packed, columns)] * 2
+        + [sds(rows, LANES)] * 2
+        + [sds(*value.shape) for value in small],
+        [HBM] * 9,
+        [VMEM] * 12,
+        [
+            pltpu.VMEM((tiles, rows, LANES), jnp.int32),
+            pltpu.SemaphoreType.DMA((tiles * planes + len(small),)),
+        ],
+        limit=8,
+    )(*[pltpu.with_memory_space_constraint(v, pltpu.HBM) for v in (initial_guess_field, medium_label, *small)])
+    near_x, far_x, near_y, far_y, *small = sends
+
+    def send(value, axis, pairs):
+        return lax.ppermute(value, axis, pairs(axis))
+
+    far_x = send(far_x, "gx", swap_far)
+    near_x = send(near_x, "gx", swap_near)
+    far_y = send(far_y, "gy", swap_far)
+    near_y = send(near_y, "gy", swap_near)
 
     table, trig, chain, size = call(
         params,
@@ -565,36 +614,31 @@
             sds(levels, 2, depth, LANES),
             sds(SUB, LANES),
         ],
-        [SMEM, VMEM, SMEM, SMEM, SMEM, SMEM, SMEM],
+        [VMEM] * 7,
         [VMEM] * 4,
         limit=4,
-    )(
-        principal_entry_addend,
-        linearized_block_weight,
-        sample_abscissae,
-        singularity_locations,
-        basis_normalizers,
-        spectral_target,
-        quasi_periodic_phase,
-    )
-
-    full, near, far = call(
-        pack_columns,
-        [sds(planes, tiles, total, LANES), sds(total, LANES), sds(total, LANES)],
-        [VMEM] * 5,
-        [VMEM] * 3,
-        limit=8,
-    )(initial_guess_field, medium_label, near, far, trig)
-    far = lax.ppermute(far, "gy", swap_far("gy"))
-    near = lax.ppermute(near, "gy", swap_near("gy"))
+    )(*small)
+
+    near_c, far_c = call(
+        pack_corners,
+        [sds(2 * HALO, LANES)] * 2,
+        [VMEM] * 2,
+        [VMEM] * 2,
+        [pltpu.VMEM((planes, 2, 2 * HALO, LANES), F32)],
+        limit=4,
+    )(near_x, far_x)
+    far_c = send(far_c, "gy", swap_far)
+    near_c = send(near_c, "gy", swap_near)
 
     wide = (tiles + 1, count, SUB, LANES)
     out, gram = call(
         solve,
         [sds(STEPS, points, 2, tiles, total, LANES), sds(devices, 1, LANES)],
-        [VMEM] * 5,
+        [VMEM] * 9,
         [VMEM] * 2,
         [
+            pltpu.VMEM((planes, tiles, total, LANES), F32),
+            pltpu.VMEM((2, total, LANES), F32),
             pltpu.VMEM((planes, total, LANES), F32),
             pltpu.VMEM((6,) + wide, F32),
             pltpu.VMEM((points, 2) + wide, F32),
@@ -602,13 +646,15 @@
             pltpu.VMEM((points, 2) + wide, F32),
         ],
         limit=32,
-    )(full, near, far, table, trig)
+    )(
+        full, near_x, far_x, near_y, far_y, near_c, far_c, table, trig
+    )
 
     part = lax.all_to_all(gram, ("gx", "gy"), 0, 0, tiled=True)
 
     basis, hess = call(
         finish,
-        [sds(points, STEPS, 2, rows, columns), sds(points, 2, names, STEPS)],
+        [sds(points, STEPS, 2, rows, columns), sds(points, STEPS, 2, names)],
         [VMEM] * 5,
         [ANY, VMEM],
         [
@@ -617,7 +663,7 @@
         ],
         limit=16,
     )(full, out, part, chain, size)
-    return basis, hess
+    return basis, hess.transpose(0, 2, 3, 1)
 
 
 def solution(mesh):

time: 43.4 us -> 40 us (0.922)
  local copies, waits for them, and re-layouts: 9.64 us -> 0 us
  blocking collectives: 9.83 us -> 11.9 us
  waiting for transfers between devices: 1.92 us -> 3.64 us
  starting transfers between devices: 8.3 us -> 9.93 us
  Pallas kernels: 12.6 us -> 13.6 us
    unnamed x18 -> x0, local copies, waits for them, and re-layouts: 8.94 us -> none
    all_to_all x1, blocking collectives: 9.83 us -> 11.9 us  [per_device(): part = lax.all_to_all(gram, ('gx', 'gy'), 0, 0, tiled=True)]
    pallas_call x3, Pallas kernels: 2.54 us -> 4.47 us  [the longest x1 2.86 us: per_device(): call(finish, [sds(points, STEPS, 2, rows, columns), sds(points, STEPS, 2,...]
    ppermute x4 -> x6, waiting for transfers between devices: 1.92 us -> 3.64 us  [send(): return lax.ppermute(value, axis, pairs(axis))]
    ppermute x4 -> x6, starting transfers between devices: 8.3 us -> 9.93 us  [send(): return lax.ppermute(value, axis, pairs(axis))]
    pallas_call x1, Pallas kernels: 1.35 us -> 0.35 us  [per_device(): call(params, [sds(8, mats, SUB, LANES), sds(points, 2, 2, SUB, LANES), sd...]
    pallas_call x1 -> x0, local copies, waits for them, and re-layouts: 0.7 us -> none  [per_device(): call(finish, [sds(points, STEPS, 2, rows, columns), sds(points, 2, names,...]
  transfers between devices with their start and end apart: 4 -> 6, of which waited for: 1 -> 3; matrix products, arithmetic and copies ran while one was open for 7% -> 0% of each run, Pallas kernels for 3% -> 1%
where the time goes in v2:
time: 40 us; the launch traced here: 39.7 us
  Pallas kernels  13.6 us (34%)
  blocking collectives  11.9 us (30%)
  starting transfers between devices  9.93 us (25%)
  waiting for transfers between devices  3.64 us (9%)
  between operations  0.7 us (2%)
    all_to_all x1, blocking collectives, per_device(): part = lax.all_to_all(gram, ('gx', 'gy'), 0, 0, tiled=True)  11.9 us
    ppermute x6, starting transfers between devices, send(): return lax.ppermute(value, axis, pairs(axis))  9.93 us
    pallas_call x1, Pallas kernels, per_device(): call(solve, [sds(STEPS, points, 2, tiles, total, LANES), sds(devices, 1,...  8.74 us
    ppermute x6, waiting for transfers between devices, send(): return lax.ppermute(value, axis, pairs(axis))  3.64 us
    pallas_call x1, Pallas kernels, per_device(): call(finish, [sds(points, STEPS, 2, rows, columns), sds(points, STEPS, 2,...  2.86 us
    pallas_call x1, Pallas kernels, per_device(): call(pack, [sds(planes, tiles, total, LANES)] + [sds(packed, columns)] *...  1.49 us
  transfers between devices with their start and end apart: 6, of which 3 were waited for; matrix products, arithmetic and copies ran while one was open for 0% of the time, Pallas kernels for 1%

profile of v2, /device:TPU:0, one launch (start us, length us, event | category | flops | bytes accessed | tf_op | source)
XLA Modules:
  0.0 39.7 jit_solution(12509753337256442244)
XLA Ops:
  0.6 1.5 %shard_map.104 = (f32[5,4,88,128]{3,2,1,0:T(8,128)S(1)}, f32[64,512]{1,0:T(8,128)S(1)}, f32[64,512]{1,0:T(8,128)S(1)}, f32[64,128]{1,0:T(8,128)S(1)}, f32[64,128...) custom-call(f32[2,2,64,512]{3,2,1,0:T(8,128)} %z_hbm.1, ...), custom_call_target="tpu_custom_call" | custom-call | tf_op jit(solution)/shard_map/pallas_call | solution.py:585
  2.1 3.0 %collective-permute-start = (f32[64,512]{1,0:T(8,128)S(1)}, f32[64,512]{1,0:T(8,128)S(1)}, u32[]{:S(2)}, u32[]{:S(2)}) collective-permute-start(f32[64,512]{1,0:T(8,128)S(1)} %get-tuple-element.25), channel_id=1, source_target_pairs={{0,4},{4,0},{8,12},{12,8},{16,20},{20,16},{24,28},{28,24},{1,5},{5... | collective-permute-start | bytes 393224 | tf_op jit(solution)/shard_map/ppermute | solution.py:602
  5.2 3.6 %collective-permute-start.1 = (f32[64,512]{1,0:T(8,128)S(1)}, f32[64,512]{1,0:T(8,128)S(1)}, u32[]{:S(2)}, u32[]{:S(2)}) collective-permute-start(f32[64,512]{1,0:T(8,128)S(1)} %get-tuple-element.26), channel_id=1, source_target_pairs={{0,28},{4,8},{8,4},{12,16},{16,12},{20,24},{24,20},{28,0},{1,29},{... | collective-permute-start | bytes 393224 | tf_op jit(solution)/shard_map/ppermute | solution.py:602
  8.7 0.0 collective-permute-start.2
  8.7 1.6 %collective-permute-start.3 = (f32[64,128]{1,0:T(8,128)S(1)}, f32[64,128]{1,0:T(8,128)S(1)}, u32[]{:S(2)}, u32[]{:S(2)}) collective-permute-start(f32[64,128]{1,0:T(8,128)S(1)} %get-tuple-element.28), channel_id=1, source_target_pairs={{0,3},{1,2},{2,1},{3,0},{4,7},{5,6},{6,5},{7,4},{8,11},{9,10},{10,... | collective-permute-start | bytes 98312 | tf_op jit(solution)/shard_map/ppermute | solution.py:602
  10.4 0.4 collective-permute-done.near_x
  10.7 2.1 %collective-permute-done.1.far_x = f32[64,512]{1,0:T(8,128)S(1)} collective-permute-done((f32[64,512]{1,0:T(8,128)S(1)}, f32[64,512]{1,0:T(8,128)S(1)}, u32[]{:S(2)}, u32[]{:S(2)}) %collective-permute-start.1) | collective-permute-done | bytes 131104 | tf_op jit(solution)/shard_map/ppermute | solution.py:602
  12.8 0.1 shard_map.105
  13.0 0.1 collective-permute-start.4
  13.0 1.6 %collective-permute-start.5 = (f32[24,128]{1,0:T(8,128)S(1)}, f32[24,128]{1,0:T(8,128)S(1)}, u32[]{:S(2)}, u32[]{:S(2)}) collective-permute-start(f32[24,128]{1,0:T(8,128)S(1)} %get-tuple-element.30), channel_id=1, source_target_pairs={{0,3},{1,2},{2,1},{3,0},{4,7},{5,6},{6,5},{7,4},{8,11},{9,10},{10,... | collective-permute-start | bytes 36872 | tf_op jit(solution)/shard_map/ppermute | solution.py:602
  14.7 0.4 shard_map.106
  15.0 0.0 collective-permute-done.2.near_y
  15.0 0.0 collective-permute-done.3.far_y
  15.0 0.0 collective-permute-done.4.near_c
  15.0 1.2 %collective-permute-done.5.far_c = f32[24,128]{1,0:T(8,128)S(1)} collective-permute-done((f32[24,128]{1,0:T(8,128)S(1)}, f32[24,128]{1,0:T(8,128)S(1)}, u32[]{:S(2)}, u32[]{:S(2)}) %collective-permute-start.5) | collective-permute-done | bytes 12320 | tf_op jit(solution)/shard_map/ppermute | solution.py:602
  16.2 8.7 %shard_map.107 = (f32[3,2,2,4,88,128]{5,4,3,2,1,0:T(8,128)S(1)}, f32[32,1,128]{2,1,0:T(1,128)S(1)}) custom-call(f32[5,4,88,128]{3,2,1,0:T(8,128)S(1)} %get-tuple-element.24.own_ref.full_ref, f32[64,512]{1,0:T(8,128)S(1)} %collective-permute-done.near_x, f32[64,512]{1,0:T(8,128)S(1)} %collective-permute-done.1.far_x, ...), custom_call_target="tpu_custom_call" | custom-call | tf_op jit(solution)/shard_map/pallas_call | solution.py:634
  25.0 11.9 %all_to_all.5.part_ref = f32[32,1,128]{2,1,0:T(1,128)S(1)} all-to-all(f32[32,1,128]{2,1,0:T(1,128)S(1)} %get-tuple-element.41), channel_id=1, replica_groups=mesh['gx'=8,'gy'=4] {'gx','gy'}, dimensions={0} | all-to-all | bytes 32768 | tf_op jit(solution)/shard_map/all_to_all | solution.py:653
  36.9 2.9 %shard_map.108 = (f32[2,3,2,64,512]{4,3,2,1,0:T(8,128)}, f32[2,3,2,4]{3,2,1,0:T(2,128)}) custom-call(f32[5,4,88,128]{3,2,1,0:T(8,128)S(1)} %get-tuple-element.24.own_ref.full_ref, f32[3,2,2,4,88,128]{5,4,3,2,1,0:T(8,128)S(1)} %get-tuple-element.40.out_ref, f32[32,1,128]{2,1,0:T(1,128)S(1)} %all_to_all.5.part_ref, ...), custom_call_target="tpu_custom_call" | custom-call | tf_op jit(solution)/shard_map/pallas_call | solution.py:655
Async XLA Ops:
  2.1 8.6 %collective-permute-start = (f32[64,512]{1,0:T(8,128)S(1)}, f32[64,512]{1,0:T(8,128)S(1)}, u32[]{:S(2)}, u32[]{:S(2)}) collective-permute-start(f32[64,512]{1,0:T(8,128)S(1)} %get-tuple-element.25), channel_id=1, source_target_pairs={{0,4},{4,0},{8,12},{12,8},{16,20},{20,16},{24,28},{28,24},{1,5},{5... | collective-permute-start | bytes 393224 | tf_op jit(solution)/shard_map/ppermute | solution.py:602
  5.2 7.7 %collective-permute-start.1 = (f32[64,512]{1,0:T(8,128)S(1)}, f32[64,512]{1,0:T(8,128)S(1)}, u32[]{:S(2)}, u32[]{:S(2)}) collective-permute-start(f32[64,512]{1,0:T(8,128)S(1)} %get-tuple-element.26), channel_id=1, source_target_pairs={{0,28},{4,8},{8,4},{12,16},{16,12},{20,24},{24,20},{28,0},{1,29},{... | collective-permute-start | bytes 393224 | tf_op jit(solution)/shard_map/ppermute | solution.py:602
  8.7 6.3 %collective-permute-start.2 = (f32[64,128]{1,0:T(8,128)S(1)}, f32[64,128]{1,0:T(8,128)S(1)}, u32[]{:S(2)}, u32[]{:S(2)}) collective-permute-start(f32[64,128]{1,0:T(8,128)S(1)} %get-tuple-element.27), channel_id=1, source_target_pairs={{0,1},{1,0},{2,3},{3,2},{4,5},{5,4},{6,7},{7,6},{8,9},{9,8},{10,11... | collective-permute-start | bytes 98312 | tf_op jit(solution)/shard_map/ppermute | solution.py:602
  8.7 6.3 %collective-permute-start.3 = (f32[64,128]{1,0:T(8,128)S(1)}, f32[64,128]{1,0:T(8,128)S(1)}, u32[]{:S(2)}, u32[]{:S(2)}) collective-permute-start(f32[64,128]{1,0:T(8,128)S(1)} %get-tuple-element.28), channel_id=1, source_target_pairs={{0,3},{1,2},{2,1},{3,0},{4,7},{5,6},{6,5},{7,4},{8,11},{9,10},{10,... | collective-permute-start | bytes 98312 | tf_op jit(solution)/shard_map/ppermute | solution.py:602
  13.0 2.1 %collective-permute-start.4 = (f32[24,128]{1,0:T(8,128)S(1)}, f32[24,128]{1,0:T(8,128)S(1)}, u32[]{:S(2)}, u32[]{:S(2)}) collective-permute-start(f32[24,128]{1,0:T(8,128)S(1)} %get-tuple-element.29), channel_id=1, source_target_pairs={{0,1},{1,0},{2,3},{3,2},{4,5},{5,4},{6,7},{7,6},{8,9},{9,8},{10,11... | collective-permute-start | bytes 36872 | tf_op jit(solution)/shard_map/ppermute | solution.py:602
  13.0 3.2 %collective-permute-start.5 = (f32[24,128]{1,0:T(8,128)S(1)}, f32[24,128]{1,0:T(8,128)S(1)}, u32[]{:S(2)}, u32[]{:S(2)}) collective-permute-start(f32[24,128]{1,0:T(8,128)S(1)} %get-tuple-element.30), channel_id=1, source_target_pairs={{0,3},{1,2},{2,1},{3,0},{4,7},{5,6},{6,5},{7,4},{8,11},{9,10},{10,... | collective-permute-start | bytes 36872 | tf_op jit(solution)/shard_map/ppermute | solution.py:602

commit v3 on v2

--- a/solution.py
+++ b/solution.py
@@ -193,31 +193,108 @@
         step = cmul(step, moved)
 
 
-def solve(own_ref, near_x, far_x, near_y, far_y, near_c, far_c,
-          table_ref, trig_ref, out_ref, gram_ref,
-          full_ref, edge_ref, halo_ref, cell_ref, b_ref, x_ref, keep_ref):
-    planes, tiles, total, _ = own_ref.shape
+def spread_lanes(tiles):
+    count = len(tiles)
+    shape = tiles[0].shape
+    lane = lax.broadcasted_iota(jnp.int32, shape, 1)
+    owner = lane // (LANES // count)
+    result = []
+    for j in range(count):
+        index = lax.rem(lane * count + j, LANES)
+        value = jnp.take_along_axis(tiles[0], index, axis=1)
+        for t in range(1, count):
+            value = jnp.where(owner == t, jnp.take_along_axis(tiles[t], index, axis=1), value)
+        result.append(value)
+    return result
+
+
+def spread(full_ref, own_ref):
+    planes, tiles, rows, _ = own_ref.shape
+    for plane in range(planes):
+        for r in range(0, rows, SUB):
+            values = spread_lanes([full_ref[plane, t, r : r + SUB, :] for t in range(tiles)])
+            for j, value in enumerate(values):
+                own_ref[plane, j, r : r + SUB, :] = value
+
+
+def picker(label, table_ref):
+    mats = table_ref.shape[1]
+    picks = [label == float(m) for m in range(1, mats)]
+
+    def pick(e):
+        value = table_ref[e, 0]
+        for m in range(1, mats):
+            value = jnp.where(picks[m - 1], table_ref[e, m], value)
+        return value
+
+    return pick
+
+
+def ends(axis):
+    first = (lax.axis_index(axis) == 0).astype(F32)
+    last = (lax.axis_index(axis) == lax.axis_size(axis) - 1).astype(F32)
+    return first, last
+
+
+def row_turns(trig_ref, k):
+    first, last = ends("gx")
+    low = lax.broadcasted_iota(jnp.int32, (2 * HALO, LANES), 0) < HALO
+    edge = jnp.where(low, last, first) > 0.5
+    sine = trig_ref[k, 0, 1][0:1, :]
+    co = jnp.where(edge, trig_ref[k, 0, 0][0:1, :], 1.0)
+    return co, jnp.where(edge, jnp.where(low, sine, -sine), 0.0)
+
+
+def stage(own_ref, near_x, far_x, table_ref, trig_ref, cell_ref, b_ref, raw_ref, work_ref):
+    planes, tiles, rows, _ = own_ref.shape
     points = planes // 2
-    rows = total - 2 * HALO
-    mats = table_ref.shape[1]
+    total = rows + 2 * HALO
     count = total // SUB
     x_even = even("gx")
-    y_even = even("gy")
-
     for plane in range(planes):
         span = slice(plane * HALO, (plane + 1) * HALO)
         for t in range(tiles):
             lanes = slice(t * LANES, (t + 1) * LANES)
             near = near_x[span, lanes]
             far = far_x[span, lanes]
-            full_ref[plane, t, 0:rows, :] = own_ref[plane, t, 0:rows, :]
-            full_ref[plane, t, rows : rows + HALO, :] = jnp.where(x_even, near, far)
-            full_ref[plane, t, rows + HALO : total, :] = jnp.where(x_even, far, near)
+            raw_ref[plane, t, 0:HALO, :] = jnp.where(x_even, near, far)
+            raw_ref[plane, t, HALO : 2 * HALO, :] = jnp.where(x_even, far, near)
+            work_ref[plane, t, 0:rows, :] = own_ref[plane, t]
+    for k in range(points):
+        turn = row_turns(trig_ref, k)
+        for t in range(tiles):
+            turned = cmul((raw_ref[2 * k, t], raw_ref[2 * k + 1, t]), turn)
+            raw_ref[2 * k, t] = turned[0]
+            raw_ref[2 * k + 1, t] = turned[1]
+    for plane in range(planes):
+        for r in range(0, 2 * HALO, SUB):
+            values = spread_lanes([raw_ref[plane, t, r : r + SUB, :] for t in range(tiles)])
+            for j, value in enumerate(values):
+                work_ref[plane, j, rows + r : rows + r + SUB, :] = value
+    for j in range(tiles):
+        for v in range(count):
+            span = pl.ds(v, SUB, stride=count)
+            pick = picker(work_ref[planes - 1, j, span, :], table_ref)
+            for n, e in enumerate((0, 1, 4, 5, 6, 7)):
+                cell_ref[n, j, v] = pick(e)
+            weight = (pick(2), pick(3))
+            for k in range(points):
+                z = (work_ref[2 * k, j, span, :], work_ref[2 * k + 1, j, span, :])
+                for c, value in enumerate(cmul(weight, z)):
+                    b_ref[k, c, j, v] = value
+
+
+def solve(own_ref, near_y, far_y, near_c, far_c, table_ref, trig_ref, cell_own, b_own,
+          out_ref, gram_ref, edge_ref, halo_ref, cell_halo, b_ref, x_ref, w_ref, keep_ref):
+    planes, tiles, rows, _ = own_ref.shape
+    points = planes // 2
+    total = rows + 2 * HALO
+    count = total // SUB
+    y_even = even("gy")
     for side in range(2):
         keep = y_even if side == 0 else jnp.logical_not(y_even)
         edge_ref[side, 0:rows, :] = jnp.where(keep, near_y[...], far_y[...])
         edge_ref[side, rows:total, :] = jnp.where(keep, near_c[...], far_c[...])
-
     lane = lax.broadcasted_iota(jnp.int32, (total, LANES), 1)
     is_right = lane < HALO
     is_left = lane >= LANES - HALO
@@ -227,123 +304,101 @@
         right = pltpu.roll(right_src, (LANES - plane * SLOT) % LANES, 1)
         left = pltpu.roll(left_src, (LANES - HALO - plane * SLOT) % LANES, 1)
         halo_ref[plane] = jnp.where(is_right, right, jnp.where(is_left, left, 0.0))
-
-    def ends(axis):
-        first = (lax.axis_index(axis) == 0).astype(F32)
-        last = (lax.axis_index(axis) == lax.axis_size(axis) - 1).astype(F32)
-        return first, last
-
-    first, last = ends("gx")
-    low = lax.broadcasted_iota(jnp.int32, (2 * HALO, LANES), 0) < HALO
-    x_edge = jnp.where(low, last, first) > 0.5
     first, last = ends("gy")
     y_edge = jnp.where(is_right, last, jnp.where(is_left, first, 0.0)) > 0.5
     for k in range(points):
-        sine = trig_ref[k, 0, 1][0:1, :]
-        co = jnp.where(x_edge, trig_ref[k, 0, 0][0:1, :], 1.0)
-        si = jnp.where(x_edge, jnp.where(low, sine, -sine), 0.0)
-        for t in range(tiles + 1):
-            if t < tiles:
-                parts = (full_ref.at[2 * k, t], full_ref.at[2 * k + 1, t])
-            else:
-                parts = (halo_ref.at[2 * k], halo_ref.at[2 * k + 1])
-            turned = cmul((parts[0][rows:total, :], parts[1][rows:total, :]), (co, si))
-            parts[0][rows:total, :] = turned[0]
-            parts[1][rows:total, :] = turned[1]
+        turned = cmul(
+            (halo_ref[2 * k, rows:total, :], halo_ref[2 * k + 1, rows:total, :]),
+            row_turns(trig_ref, k),
+        )
+        halo_ref[2 * k, rows:total, :] = turned[0]
+        halo_ref[2 * k + 1, rows:total, :] = turned[1]
         sine = trig_ref[k, 1, 1][0:1, :]
         co = jnp.where(y_edge, trig_ref[k, 1, 0][0:1, :], 1.0)
         si = jnp.where(y_edge, jnp.where(is_right, sine, -sine), 0.0)
         turned = cmul((halo_ref[2 * k], halo_ref[2 * k + 1]), (co, si))
         halo_ref[2 * k] = turned[0]
         halo_ref[2 * k + 1] = turned[1]
-
-    def rows_of(plane, t, v):
+    for v in range(count):
         span = pl.ds(v, SUB, stride=count)
-        if t < tiles:
-            return full_ref[plane, t, span, :]
-        return halo_ref[plane, span, :]
-
-    for t in range(tiles + 1):
-        for v in range(count):
-            label = rows_of(planes - 1, t, v)
-            picks = [label == float(m) for m in range(1, mats)]
-
-            def pick(e):
-                value = table_ref[e, 0]
-                for m in range(1, mats):
-                    value = jnp.where(picks[m - 1], table_ref[e, m], value)
-                return value
-
-            for e in (0, 1):
-                cell_ref[e, t, v] = pick(e)
-            for e in (4, 5, 6, 7):
-                cell_ref[e - 2, t, v] = pick(e)
-            weight = (pick(2), pick(3))
-            for k in range(points):
-                z = (rows_of(2 * k, t, v), rows_of(2 * k + 1, t, v))
-                for c, value in enumerate(cmul(weight, z)):
-                    b_ref[k, c, t, v] = value
-                    x_ref[0, k, c, t, v] = value
+        pick = picker(halo_ref[planes - 1, span, :], table_ref)
+        for n, e in enumerate((0, 1, 4, 5, 6, 7)):
+            cell_halo[n, v] = pick(e)
+        weight = (pick(2), pick(3))
+        for k in range(points):
+            z = (halo_ref[2 * k, span, :], halo_ref[2 * k + 1, span, :])
+            for c, value in enumerate(cmul(weight, z)):
+                b_ref[k, c, tiles, v] = value
+                x_ref[k, c, tiles, v] = value
+                for t in range(tiles):
+                    own = b_own[k, c, t, v]
+                    b_ref[k, c, t, v] = own
+                    x_ref[k, c, t, v] = own
+
+    def cell(e, t, v):
+        return cell_own[e, t, v] if t < tiles else cell_halo[e, v]
 
     lane8 = lax.broadcasted_iota(jnp.int32, (SUB, LANES), 1)
     at_first = lane8 == 0
     at_last = lane8 == LANES - 1
 
-    def sweep(i, carry):
-        src = lax.rem(i, 2)
-        dst = 1 - src
+    def sweep(src_ref, dst_ref):
         for k in range(points):
             for v in range(count):
                 sides = []
                 for c in range(2):
-                    mine = [x_ref[src, k, c, t, v] for t in range(tiles + 1)]
-                    ahead = [pltpu.roll(value, 1, 1) for value in mine]
-                    behind = [pltpu.roll(value, LANES - 1, 1) for value in mine]
-                    side = []
-                    for t in range(tiles + 1):
-                        one = jnp.where(at_first, ahead[t - 1], ahead[t])
-                        two = jnp.where(at_last, behind[(t + 1) % (tiles + 1)], behind[t])
-                        side.append(one + two)
-                    sides.append(side)
+                    x = [src_ref[k, c, t, v] for t in range(tiles + 1)]
+                    last_on = pltpu.roll(x[tiles - 1], 1, 1)
+                    halo_on = pltpu.roll(x[tiles], 1, 1)
+                    first_back = pltpu.roll(x[0], LANES - 1, 1)
+                    halo_back = pltpu.roll(x[tiles], LANES - 1, 1)
+                    left = [jnp.where(at_first, halo_on, last_on)] + x[: tiles - 1]
+                    right = x[1:tiles] + [jnp.where(at_last, halo_back, first_back)]
+                    side = [a + b for a, b in zip(left, right)]
+                    one = jnp.where(at_first, last_on, halo_on)
+                    two = jnp.where(at_last, first_back, halo_back)
+                    sides.append(side + [one + two])
                 for t in range(tiles + 1):
                     n = []
                     for c in range(2):
                         if v > 0:
-                            up = x_ref[src, k, c, t, v - 1]
+                            up = src_ref[k, c, t, v - 1]
                         else:
-                            up = pltpu.roll(x_ref[src, k, c, t, count - 1], 1, 0)
+                            up = pltpu.roll(src_ref[k, c, t, count - 1], 1, 0)
                         if v < count - 1:
-                            down = x_ref[src, k, c, t, v + 1]
+                            down = src_ref[k, c, t, v + 1]
                         else:
-                            down = pltpu.roll(x_ref[src, k, c, t, 0], SUB - 1, 0)
+                            down = pltpu.roll(src_ref[k, c, t, 0], SUB - 1, 0)
                         n.append(sides[c][t] + (up + down))
-                    inverse = (cell_ref[0, t, v], cell_ref[1, t, v])
-                    n = cmul(inverse, n)
+                    n = cmul((cell(0, t, v), cell(1, t, v)), n)
                     for c in range(2):
-                        x_ref[dst, k, c, t, v] = b_ref[k, c, t, v] + n[c]
+                        dst_ref[k, c, t, v] = b_ref[k, c, t, v] + n[c]
+
+    def pair(i, carry):
+        sweep(x_ref, w_ref)
+        sweep(w_ref, x_ref)
         return carry
 
     for s in range(STEPS):
-        lax.fori_loop(0, SWEEPS, sweep, 0)
-        final = SWEEPS % 2
+        lax.fori_loop(0, SWEEPS // 2, pair, 0)
         for k in range(points):
             for t in range(tiles + 1):
                 for v in range(count):
-                    y = (x_ref[final, k, 0, t, v], x_ref[final, k, 1, t, v])
+                    y = (x_ref[k, 0, t, v], x_ref[k, 1, t, v])
                     if t < tiles:
                         for c in range(2):
                             out_ref[s, k, c, t, pl.ds(v, SUB, stride=count), :] = y[c]
                     if s < STEPS - 1:
-                        b = cmul((cell_ref[2, t, v], cell_ref[3, t, v]), y)
+                        b = cmul((cell(2, t, v), cell(3, t, v)), y)
                         if s == 0:
-                            keep = cmul((cell_ref[4, t, v], cell_ref[5, t, v]), y)
+                            keep = cmul((cell(4, t, v), cell(5, t, v)), y)
                             for c in range(2):
                                 keep_ref[k, c, t, v] = keep[c]
                         else:
                             b = cadd(b, (keep_ref[k, 0, t, v], keep_ref[k, 1, t, v]))
                         for c in range(2):
                             b_ref[k, c, t, v] = b[c]
-                            x_ref[0, k, c, t, v] = b[c]
+                            x_ref[k, c, t, v] = b[c]
 
     names = STEPS + 1
     zero = jnp.zeros((SUB, LANES), F32)
@@ -356,7 +411,7 @@
             accs = list(accs)
             span = pl.ds(pl.multiple_of(r * SUB, SUB), SUB)
             for t in range(tiles):
-                fields = [(full_ref[2 * k, t, span, :], full_ref[2 * k + 1, t, span, :])]
+                fields = [(own_ref[2 * k, t, span, :], own_ref[2 * k + 1, t, span, :])]
                 for s in range(STEPS):
                     fields.append((out_ref[s, k, 0, t, span, :], out_ref[s, k, 1, t, span, :]))
                 at = 0
@@ -379,10 +434,10 @@
     gram_ref[...] = jnp.broadcast_to(line[None], gram_ref.shape)
 
 
-def finish(full_ref, out_ref, part_ref, chain_ref, size_ref, basis_ref, hess_ref, done_ref, sem):
-    planes, tiles, total, _ = full_ref.shape
+def finish(own_ref, out_ref, part_ref, chain_ref, size_ref, basis_ref, hess_ref,
+           found_ref, turn_ref, done_ref, sem):
+    planes, tiles, rows, _ = own_ref.shape
     points = planes // 2
-    rows = total - 2 * HALO
     names = STEPS + 1
     shape = (SUB, LANES)
     line = jnp.sum(part_ref[:, 0, :], axis=0, keepdims=True)
@@ -420,8 +475,7 @@
         def combine(r, carry):
             span = pl.ds(pl.multiple_of(r * SUB, SUB), SUB)
             for t in range(tiles):
-                lanes = slice(t * LANES, (t + 1) * LANES)
-                fields = [(full_ref[2 * k, t, span, :], full_ref[2 * k + 1, t, span, :])]
+                fields = [(own_ref[2 * k, t, span, :], own_ref[2 * k + 1, t, span, :])]
                 for s in range(STEPS):
                     fields.append((out_ref[s, k, 0, t, span, :], out_ref[s, k, 1, t, span, :]))
                 found = []
@@ -432,14 +486,23 @@
                     value = (value[0] * inv[i], value[1] * inv[i])
                     found.append(value)
                     if i > 0:
-                        done_ref[k, i - 1, 0, span, lanes] = value[0]
-                        done_ref[k, i - 1, 1, span, lanes] = value[1]
+                        for c in range(2):
+                            place = pl.ds(pl.multiple_of(c * rows + r * SUB, SUB), SUB)
+                            found_ref[i - 1, t, place, :] = value[c]
             return carry
 
         lax.fori_loop(0, rows // SUB, combine, 0)
-        copy = pltpu.make_async_copy(done_ref.at[k], basis_ref.at[k], sem.at[k])
-        copy.start()
-        copies.append(copy)
+        for i in range(STEPS):
+            for n in range(0, 2 * rows, LANES):
+                for t in range(tiles):
+                    turned = found_ref[i, t, n : n + LANES, :].T
+                    turn_ref[i, pl.ds(t, LANES, stride=tiles), :] = turned
+                for t in range(tiles):
+                    lanes = slice(t * LANES, (t + 1) * LANES)
+                    done_ref[k, i, n : n + LANES, lanes] = turn_ref[i, lanes, :].T
+            copy = pltpu.make_async_copy(done_ref.at[k, i], basis_ref.at[k, i], sem.at[k, i])
+            copy.start()
+            copies.append(copy)
 
     lane = lax.broadcasted_iota(jnp.int32, shape, 1)
 
@@ -619,6 +682,8 @@
         limit=4,
     )(*small)
 
+    own = call(spread, sds(planes, tiles, rows, LANES), [VMEM], VMEM, limit=4)(full)
+
     near_c, far_c = call(
         pack_corners,
         [sds(2 * HALO, LANES)] * 2,
@@ -630,6 +695,19 @@
     far_c = send(far_c, "gy", swap_far)
     near_c = send(near_c, "gy", swap_near)
 
+    narrow = (tiles, count, SUB, LANES)
+    cell, b = call(
+        stage,
+        [sds(6, *narrow), sds(points, 2, *narrow)],
+        [VMEM] * 5,
+        [VMEM] * 2,
+        [
+            pltpu.VMEM((planes, tiles, 2 * HALO, LANES), F32),
+            pltpu.VMEM((planes, tiles, total, LANES), F32),
+        ],
+        limit=8,
+    )(own, near_x, far_x, table, trig)
+
     wide = (tiles + 1, count, SUB, LANES)
     out, gram = call(
         solve,
@@ -637,32 +715,30 @@
         [VMEM] * 9,
         [VMEM] * 2,
         [
-            pltpu.VMEM((planes, tiles, total, LANES), F32),
             pltpu.VMEM((2, total, LANES), F32),
             pltpu.VMEM((planes, total, LANES), F32),
-            pltpu.VMEM((6,) + wide, F32),
-            pltpu.VMEM((points, 2) + wide, F32),
-            pltpu.VMEM((2, points, 2) + wide, F32),
-            pltpu.VMEM((points, 2) + wide, F32),
-        ],
+            pltpu.VMEM((6,) + wide[1:], F32),
+        ]
+        + [pltpu.VMEM((points, 2) + wide, F32)] * 4,
         limit=32,
-    )(
-        full, near_x, far_x, near_y, far_y, near_c, far_c, table, trig
-    )
+    )(own, near_y, far_y, near_c, far_c, table, trig, cell, b)
 
     part = lax.all_to_all(gram, ("gx", "gy"), 0, 0, tiled=True)
 
     basis, hess = call(
         finish,
-        [sds(points, STEPS, 2, rows, columns), sds(points, STEPS, 2, names)],
+        [sds(points, STEPS, 2 * rows, columns), sds(points, STEPS, 2, names)],
         [VMEM] * 5,
         [ANY, VMEM],
         [
-            pltpu.VMEM((points, STEPS, 2, rows, columns), F32),
-            pltpu.SemaphoreType.DMA((points,)),
+            pltpu.VMEM((STEPS, tiles, 2 * rows, LANES), F32),
+            pltpu.VMEM((STEPS, columns, LANES), F32),
+            pltpu.VMEM((points, STEPS, 2 * rows, columns), F32),
+            pltpu.SemaphoreType.DMA((points, STEPS)),
         ],
         limit=16,
-    )(full, out, part, chain, size)
+    )(own, out, part, chain, size)
+    basis = basis.reshape(points, STEPS, 2, rows, columns)
     return basis, hess.transpose(0, 2, 3, 1)
 
 

time: 40 us -> 36.6 us (0.915)
  Pallas kernels: 13.6 us -> 12.2 us
  waiting for transfers between devices: 3.64 us -> 2.47 us
  blocking collectives: 11.9 us -> 11 us
    pallas_call x1, Pallas kernels: 8.74 us -> 4.71 us  [per_device(): call(solve, [sds(STEPS, points, 2, tiles, total, LANES), sds(devices, 1,...]
    pallas_call x1 -> x3, Pallas kernels: 2.86 us -> 5.56 us  [the longest x1 3.53 us: per_device(): call(finish, [sds(points, STEPS, 2 * rows, columns), sds(points, STEPS, 2...]
    ppermute x6, waiting for transfers between devices: 3.64 us -> 2.47 us  [send(): return lax.ppermute(value, axis, pairs(axis))]
    all_to_all x1, blocking collectives: 11.9 us -> 11 us  [per_device(): part = lax.all_to_all(gram, ('gx', 'gy'), 0, 0, tiled=True)]
  transfers between devices with their start and end apart: 6 -> 6, of which waited for: 3 -> 2; matrix products, arithmetic and copies ran while one was open for 0% -> 0% of each run, Pallas kernels for 1% -> 7%
where the time goes in v3:
time: 36.6 us; the launch traced here: 36.4 us
  Pallas kernels  12.2 us (33%)
  blocking collectives  11 us (30%)
  starting transfers between devices  9.93 us (27%)
  waiting for transfers between devices  2.47 us (7%)
  between operations  0.72 us (2%)
    all_to_all x1, blocking collectives, per_device(): part = lax.all_to_all(gram, ('gx', 'gy'), 0, 0, tiled=True)  11 us
    ppermute x6, starting transfers between devices, send(): return lax.ppermute(value, axis, pairs(axis))  9.93 us
    pallas_call x1, Pallas kernels, per_device(): call(solve, [sds(STEPS, points, 2, tiles, total, LANES), sds(devices, 1,...  4.71 us
    pallas_call x1, Pallas kernels, per_device(): call(finish, [sds(points, STEPS, 2 * rows, columns), sds(points, STEPS, 2...  3.53 us
    ppermute x6, waiting for transfers between devices, send(): return lax.ppermute(value, axis, pairs(axis))  2.47 us
    pallas_call x1, Pallas kernels, per_device(): call(pack, [sds(planes, tiles, total, LANES)] + [sds(packed, columns)] *...  1.49 us
    pallas_call x1, Pallas kernels, per_device(): call(spread, sds(planes, tiles, rows, LANES), [VMEM], VMEM, limit=4)(full)  1.25 us
    pallas_call x1, Pallas kernels, per_device(): call(stage, [sds(6, *narrow), sds(points, 2, *narrow)], [VMEM] * 5, [VMEM...  0.78 us
  transfers between devices with their start and end apart: 6, of which 2 were waited for; matrix products, arithmetic and copies ran while one was open for 0% of the time, Pallas kernels for 7%

profile of v3, /device:TPU:0, one launch (start us, length us, event | category | flops | bytes accessed | tf_op | source)
XLA Modules:
  0.0 36.4 jit_solution(15681335851273915397)
XLA Ops:
  0.6 1.5 %shard_map.104 = (f32[5,4,88,128]{3,2,1,0:T(8,128)S(1)}, f32[64,512]{1,0:T(8,128)S(1)}, f32[64,512]{1,0:T(8,128)S(1)}, f32[64,128]{1,0:T(8,128)S(1)}, f32[64,128...) custom-call(f32[2,2,64,512]{3,2,1,0:T(8,128)} %z_hbm.1, ...), custom_call_target="tpu_custom_call" | custom-call | tf_op jit(solution)/shard_map/pallas_call | solution.py:648
  2.1 3.0 %collective-permute-start.2 = (f32[64,512]{1,0:T(8,128)S(1)}, f32[64,512]{1,0:T(8,128)S(1)}, u32[]{:S(2)}, u32[]{:S(2)}) collective-permute-start(f32[64,512]{1,0:T(8,128)S(1)} %get-tuple-element.29), channel_id=1, source_target_pairs={{0,4},{4,0},{8,12},{12,8},{16,20},{20,16},{24,28},{28,24},{1,5},{5... | collective-permute-start | bytes 393224 | tf_op jit(solution)/shard_map/ppermute | solution.py:665
  5.2 3.6 %collective-permute-start.3 = (f32[64,512]{1,0:T(8,128)S(1)}, f32[64,512]{1,0:T(8,128)S(1)}, u32[]{:S(2)}, u32[]{:S(2)}) collective-permute-start(f32[64,512]{1,0:T(8,128)S(1)} %get-tuple-element.30), channel_id=1, source_target_pairs={{0,28},{4,8},{8,4},{12,16},{16,12},{20,24},{24,20},{28,0},{1,29},{... | collective-permute-start | bytes 393224 | tf_op jit(solution)/shard_map/ppermute | solution.py:665
  8.7 0.0 collective-permute-start
  8.7 1.6 %collective-permute-start.1 = (f32[64,128]{1,0:T(8,128)S(1)}, f32[64,128]{1,0:T(8,128)S(1)}, u32[]{:S(2)}, u32[]{:S(2)}) collective-permute-start(f32[64,128]{1,0:T(8,128)S(1)} %get-tuple-element.28), channel_id=1, source_target_pairs={{0,3},{1,2},{2,1},{3,0},{4,7},{5,6},{6,5},{7,4},{8,11},{9,10},{10,... | collective-permute-start | bytes 98312 | tf_op jit(solution)/shard_map/ppermute | solution.py:665
  10.4 0.4 collective-permute-done.2.near_x
  10.7 2.1 %collective-permute-done.3.far_x = f32[64,512]{1,0:T(8,128)S(1)} collective-permute-done((f32[64,512]{1,0:T(8,128)S(1)}, f32[64,512]{1,0:T(8,128)S(1)}, u32[]{:S(2)}, u32[]{:S(2)}) %collective-permute-start.3) | collective-permute-done | bytes 131104 | tf_op jit(solution)/shard_map/ppermute | solution.py:665
  12.8 0.1 shard_map.106
  13.0 0.1 collective-permute-start.4
  13.0 1.6 %collective-permute-start.5 = (f32[24,128]{1,0:T(8,128)S(1)}, f32[24,128]{1,0:T(8,128)S(1)}, u32[]{:S(2)}, u32[]{:S(2)}) collective-permute-start(f32[24,128]{1,0:T(8,128)S(1)} %get-tuple-element.32), channel_id=1, source_target_pairs={{0,3},{1,2},{2,1},{3,0},{4,7},{5,6},{6,5},{7,4},{8,11},{9,10},{10,... | collective-permute-start | bytes 36872 | tf_op jit(solution)/shard_map/ppermute | solution.py:665
  14.7 1.3 %shard_map.105.own_ref = f32[5,4,64,128]{3,2,1,0:T(8,128)S(1)} custom-call(f32[5,4,88,128]{3,2,1,0:T(8,128)S(1)} %get-tuple-element.26.full_ref), custom_call_target="tpu_custom_call" | custom-call | tf_op jit(solution)/shard_map/pallas_call | solution.py:685
  15.9 0.4 %shard_map.107 = (f32[8,4,8,128]{3,2,1,0:T(8,128)S(1)}, f32[2,2,2,8,128]{4,3,2,1,0:T(8,128)S(1)}, f32[5,2,32,128]{3,2,1,0:T(8,128)S(1)}, f32[8,128]{1,0:T(8,128)S(1)}) custom-call(f32[2,4]{1,0:T(2,128)S(1)} %get-tuple-element.33.a_ref, f32[4,2,25]{2,1,0:T(2,128)S(1)} %get-tuple-element.34.w_ref, f32[2,24]{1,0:T(2,128)S(1)} %get-tuple-element.35.node_ref, ...), custom_call_target="tpu_custom_call" | custom-call | tf_op jit(solution)/shard_map/pallas_call | solution.py:672
  16.3 0.8 %shard_map.108 = (f32[6,4,11,8,128]{4,3,2,1,0:T(8,128)S(1)}, f32[2,2,4,11,8,128]{5,4,3,2,1,0:T(8,128)S(1)}) custom-call(f32[5,4,64,128]{3,2,1,0:T(8,128)S(1)} %shard_map.105.own_ref, f32[64,512]{1,0:T(8,128)S(1)} %collective-permute-done.2.near_x, f32[64,512]{1,0:T(8,128)S(1)} %collective-permute-done.3.far_x, ...), custom_call_target="tpu_custom_call" | custom-call | tf_op jit(solution)/shard_map/pallas_call | solution.py:699
  17.1 0.0 collective-permute-done.near_y
  17.1 0.0 collective-permute-done.1.far_y
  17.1 0.0 collective-permute-done.4.near_c
  17.1 0.0 collective-permute-done.5.far_c
  17.1 4.7 %shard_map.109 = (f32[3,2,2,4,88,128]{5,4,3,2,1,0:T(8,128)S(1)}, f32[32,1,128]{2,1,0:T(1,128)S(1)}) custom-call(f32[5,4,64,128]{3,2,1,0:T(8,128)S(1)} %shard_map.105.own_ref, f32[64,128]{1,0:T(8,128)S(1)} %collective-permute-done.near_y, f32[64,128]{1,0:T(8,128)S(1)} %collective-permute-done.1.far_y, f32[24,128]{1,0:T(8,128)S(1)} %collective-permute-done.4.near_c, ...), custom_call_target="tpu_custom_call" | custom-call | tf_op jit(solution)/shard_map/pallas_call | solution.py:712
  21.8 11.0 %all_to_all.5.part_ref = f32[32,1,128]{2,1,0:T(1,128)S(1)} all-to-all(f32[32,1,128]{2,1,0:T(1,128)S(1)} %get-tuple-element.45), channel_id=1, replica_groups=mesh['gx'=8,'gy'=4] {'gx','gy'}, dimensions={0} | all-to-all | bytes 32768 | tf_op jit(solution)/shard_map/all_to_all | solution.py:726
  32.8 3.5 %shard_map.110 = (f32[2,3,128,512]{3,2,1,0:T(8,128)}, f32[2,3,2,4]{3,2,1,0:T(2,128)}) custom-call(f32[5,4,64,128]{3,2,1,0:T(8,128)S(1)} %shard_map.105.own_ref, f32[3,2,2,4,88,128]{5,4,3,2,1,0:T(8,128)S(1)} %get-tuple-element.44.out_ref, f32[32,1,128]{2,1,0:T(1,128)S(1)} %all_to_all.5.part_ref, f32[5,2,32,128]{3,2,1,0:T(8,128)S(1)} %get-tuple-element.46.chain_ref, ...), custom_call_target="tpu_custom_call" | custom-call | tf_op jit(solution)/shard_map/pallas_call | solution.py:728
Async XLA Ops:
  2.1 8.6 %collective-permute-start.2 = (f32[64,512]{1,0:T(8,128)S(1)}, f32[64,512]{1,0:T(8,128)S(1)}, u32[]{:S(2)}, u32[]{:S(2)}) collective-permute-start(f32[64,512]{1,0:T(8,128)S(1)} %get-tuple-element.29), channel_id=1, source_target_pairs={{0,4},{4,0},{8,12},{12,8},{16,20},{20,16},{24,28},{28,24},{1,5},{5... | collective-permute-start | bytes 393224 | tf_op jit(solution)/shard_map/ppermute | solution.py:665
  5.2 7.7 %collective-permute-start.3 = (f32[64,512]{1,0:T(8,128)S(1)}, f32[64,512]{1,0:T(8,128)S(1)}, u32[]{:S(2)}, u32[]{:S(2)}) collective-permute-start(f32[64,512]{1,0:T(8,128)S(1)} %get-tuple-element.30), channel_id=1, source_target_pairs={{0,28},{4,8},{8,4},{12,16},{16,12},{20,24},{24,20},{28,0},{1,29},{... | collective-permute-start | bytes 393224 | tf_op jit(solution)/shard_map/ppermute | solution.py:665
  8.7 8.3 %collective-permute-start = (f32[64,128]{1,0:T(8,128)S(1)}, f32[64,128]{1,0:T(8,128)S(1)}, u32[]{:S(2)}, u32[]{:S(2)}) collective-permute-start(f32[64,128]{1,0:T(8,128)S(1)} %get-tuple-element.27), channel_id=1, source_target_pairs={{0,1},{1,0},{2,3},{3,2},{4,5},{5,4},{6,7},{7,6},{8,9},{9,8},{10,11... | collective-permute-start | bytes 98312 | tf_op jit(solution)/shard_map/ppermute | solution.py:665
  8.7 8.3 %collective-permute-start.1 = (f32[64,128]{1,0:T(8,128)S(1)}, f32[64,128]{1,0:T(8,128)S(1)}, u32[]{:S(2)}, u32[]{:S(2)}) collective-permute-start(f32[64,128]{1,0:T(8,128)S(1)} %get-tuple-element.28), channel_id=1, source_target_pairs={{0,3},{1,2},{2,1},{3,0},{4,7},{5,6},{6,5},{7,4},{8,11},{9,10},{10,... | collective-permute-start | bytes 98312 | tf_op jit(solution)/shard_map/ppermute | solution.py:665
  13.0 4.1 %collective-permute-start.4 = (f32[24,128]{1,0:T(8,128)S(1)}, f32[24,128]{1,0:T(8,128)S(1)}, u32[]{:S(2)}, u32[]{:S(2)}) collective-permute-start(f32[24,128]{1,0:T(8,128)S(1)} %get-tuple-element.31), channel_id=1, source_target_pairs={{0,1},{1,0},{2,3},{3,2},{4,5},{5,4},{6,7},{7,6},{8,9},{9,8},{10,11... | collective-permute-start | bytes 36872 | tf_op jit(solution)/shard_map/ppermute | solution.py:665
  13.0 4.1 %collective-permute-start.5 = (f32[24,128]{1,0:T(8,128)S(1)}, f32[24,128]{1,0:T(8,128)S(1)}, u32[]{:S(2)}, u32[]{:S(2)}) collective-permute-start(f32[24,128]{1,0:T(8,128)S(1)} %get-tuple-element.32), channel_id=1, source_target_pairs={{0,3},{1,2},{2,1},{3,0},{4,7},{5,6},{6,5},{7,4},{8,11},{9,10},{10,... | collective-permute-start | bytes 36872 | tf_op jit(solution)/shard_map/ppermute | solution.py:665

commit v4 on v3

--- a/solution.py
+++ b/solution.py
@@ -12,6 +12,7 @@
 LANES = 128
 SUB = 8
 SLOT = 16
+STRIP = 16
 F32 = jnp.float32
 VMEM = pl.BlockSpec(memory_space=pltpu.VMEM)
 SMEM = pl.BlockSpec(memory_space=pltpu.SMEM)
@@ -81,10 +82,41 @@
     near_c[...], far_c[...] = pack_lanes([(side_ref[p, 0], side_ref[p, 1]) for p in range(planes)])
 
 
-def pack(z_hbm, m_hbm, a_hbm, w_hbm, node_hbm, pole_hbm, scale_hbm, target_hbm, phase_hbm,
-         full_ref, near_x, far_x, near_y, far_y,
+def run_copies(pairs, sem):
+    copies = [pltpu.make_async_copy(src, dst, sem.at[n]) for n, (src, dst) in enumerate(pairs)]
+    for copy in copies:
+        copy.start()
+    for copy in copies:
+        copy.wait()
+
+
+def pack_rows(z_hbm, m_hbm, near_x, far_x, strip_ref, label_ref, sem):
+    points, _, rows, _ = z_hbm.shape
+    pairs = []
+    for side, at in enumerate((0, rows - STRIP)):
+        span = pl.ds(at, STRIP)
+        for plane in range(2 * points):
+            src = z_hbm.at[plane // 2, plane % 2, span, :]
+            pairs.append((src, strip_ref.at[plane, side]))
+        pairs.append((m_hbm.at[span, :], label_ref.at[side]))
+    run_copies(pairs, sem)
+    x_even = even("gx")
+    for plane in range(2 * points + 1):
+        if plane < 2 * points:
+            top = strip_ref[plane, 0, 0:HALO, :]
+            bottom = strip_ref[plane, 1, STRIP - HALO : STRIP, :]
+        else:
+            top = label_ref[0, 0:HALO, :].astype(F32)
+            bottom = label_ref[1, STRIP - HALO : STRIP, :].astype(F32)
+        span = slice(plane * HALO, (plane + 1) * HALO)
+        near_x[span, :] = jnp.where(x_even, bottom, top)
+        far_x[span, :] = jnp.where(x_even, top, bottom)
+
+
+def load(z_hbm, m_hbm, a_hbm, w_hbm, node_hbm, pole_hbm, scale_hbm, target_hbm, phase_hbm,
+         full_ref, near_y, far_y,
          a_ref, w_ref, node_ref, pole_ref, scale_ref, target_ref, phase_ref, label_ref, sem):
-    points, _, rows, columns = z_hbm.shape
+    points, _, _, columns = z_hbm.shape
     tiles = columns // LANES
     planes = 2 * points + 1
     pairs = []
@@ -92,30 +124,15 @@
         lanes = pl.ds(t * LANES, LANES)
         for plane in range(2 * points):
             src = z_hbm.at[plane // 2, plane % 2, :, lanes]
-            pairs.append((src, full_ref.at[plane, t, pl.ds(0, rows), :]))
+            pairs.append((src, full_ref.at[plane, t]))
         pairs.append((m_hbm.at[:, lanes], label_ref.at[t]))
     pairs += [(a_hbm, a_ref), (w_hbm, w_ref), (node_hbm, node_ref), (pole_hbm, pole_ref)]
     pairs += [(scale_hbm, scale_ref), (target_hbm, target_ref), (phase_hbm, phase_ref)]
-    copies = [pltpu.make_async_copy(src, dst, sem.at[n]) for n, (src, dst) in enumerate(pairs)]
-    for copy in copies:
-        copy.start()
-    for copy in copies:
-        copy.wait()
+    run_copies(pairs, sem)
     for t in range(tiles):
-        full_ref[planes - 1, t, 0:rows, :] = label_ref[t].astype(F32)
-    x_even = even("gx")
-    sides = [(full_ref[p, 0, 0:rows, :], full_ref[p, tiles - 1, 0:rows, :]) for p in range(planes)]
-    near_acc, far_acc = pack_lanes(sides)
-    near_y[...] = near_acc
-    far_y[...] = far_acc
-    for plane in range(planes):
-        span = slice(plane * HALO, (plane + 1) * HALO)
-        for t in range(tiles):
-            lanes = slice(t * LANES, (t + 1) * LANES)
-            top = full_ref[plane, t, 0:HALO, :]
-            bottom = full_ref[plane, t, rows - HALO : rows, :]
-            near_x[span, lanes] = jnp.where(x_even, bottom, top)
-            far_x[span, lanes] = jnp.where(x_even, top, bottom)
+        full_ref[planes - 1, t] = label_ref[t].astype(F32)
+    sides = [(full_ref[p, 0], full_ref[p, tiles - 1]) for p in range(planes)]
+    near_y[...], far_y[...] = pack_lanes(sides)
 
 
 def params(a_ref, w_ref, node_ref, pole_ref, scale_ref, target_ref, phase_ref,
@@ -434,8 +451,8 @@
     gram_ref[...] = jnp.broadcast_to(line[None], gram_ref.shape)
 
 
-def finish(own_ref, out_ref, part_ref, chain_ref, size_ref, basis_ref, hess_ref,
-           found_ref, turn_ref, done_ref, sem):
+def finish(own_ref, out_ref, part_ref, chain_ref, size_ref, basis_ref, hess_out,
+           found_ref, turn_ref, done_ref, hess_ref, sem, hess_sem):
     planes, tiles, rows, _ = own_ref.shape
     points = planes // 2
     names = STEPS + 1
@@ -472,37 +489,45 @@
         uppers.append(upper)
         inverses.append(inv)
 
-        def combine(r, carry):
-            span = pl.ds(pl.multiple_of(r * SUB, SUB), SUB)
-            for t in range(tiles):
-                fields = [(own_ref[2 * k, t, span, :], own_ref[2 * k + 1, t, span, :])]
-                for s in range(STEPS):
-                    fields.append((out_ref[s, k, 0, t, span, :], out_ref[s, k, 1, t, span, :]))
-                found = []
-                for i in range(names):
-                    value = fields[i]
-                    for l in range(i):
-                        value = csub(value, cmul(upper[l, i], found[l]))
-                    value = (value[0] * inv[i], value[1] * inv[i])
-                    found.append(value)
-                    if i > 0:
-                        for c in range(2):
-                            place = pl.ds(pl.multiple_of(c * rows + r * SUB, SUB), SUB)
-                            found_ref[i - 1, t, place, :] = value[c]
-            return carry
-
-        lax.fori_loop(0, rows // SUB, combine, 0)
+    def combine(k, r):
+        upper = uppers[k]
+        inv = inverses[k]
+        span = slice(r * SUB, (r + 1) * SUB)
+        for t in range(tiles):
+            fields = [(own_ref[2 * k, t, span, :], own_ref[2 * k + 1, t, span, :])]
+            for s in range(STEPS):
+                fields.append((out_ref[s, k, 0, t, span, :], out_ref[s, k, 1, t, span, :]))
+            found = []
+            for i in range(names):
+                value = fields[i]
+                for l in range(i):
+                    value = csub(value, cmul(upper[l, i], found[l]))
+                value = (value[0] * inv[i], value[1] * inv[i])
+                found.append(value)
+                if i > 0:
+                    for c in range(2):
+                        place = slice(c * rows + r * SUB, c * rows + (r + 1) * SUB)
+                        found_ref[k, i - 1, t, place, :] = value[c]
+
+    piece = 32
+    for k in range(points):
+        for r in range(rows // SUB):
+            combine(k, r)
         for i in range(STEPS):
             for n in range(0, 2 * rows, LANES):
                 for t in range(tiles):
-                    turned = found_ref[i, t, n : n + LANES, :].T
-                    turn_ref[i, pl.ds(t, LANES, stride=tiles), :] = turned
+                    turned = found_ref[k, i, t, n : n + LANES, :].T
+                    turn_ref[k, i, pl.ds(t, LANES, stride=tiles), :] = turned
                 for t in range(tiles):
                     lanes = slice(t * LANES, (t + 1) * LANES)
-                    done_ref[k, i, n : n + LANES, lanes] = turn_ref[i, lanes, :].T
-            copy = pltpu.make_async_copy(done_ref.at[k, i], basis_ref.at[k, i], sem.at[k, i])
-            copy.start()
-            copies.append(copy)
+                    done_ref[k, i, n : n + LANES, lanes] = turn_ref[k, i, lanes, :].T
+            for at, n in enumerate(range(0, 2 * rows, piece)):
+                part = pl.ds(n, piece)
+                copy = pltpu.make_async_copy(
+                    done_ref.at[k, i, part, :], basis_ref.at[k, i, part, :], sem.at[k, i, at]
+                )
+                copy.start()
+                copies.append(copy)
 
     lane = lax.broadcasted_iota(jnp.int32, shape, 1)
 
@@ -597,6 +622,9 @@
                     here = (part_row == c) & (part_lane == j)
                     value = jnp.where(here, entry[0:1, p : p + 1], value)
             hess_ref[p, k] = value
+    copy = pltpu.make_async_copy(hess_ref, hess_out, hess_sem)
+    copy.start()
+    copies.append(copy)
     for copy in copies:
         copy.wait()
 
@@ -645,27 +673,40 @@
         spectral_target.reshape(1, -1),
         quasi_periodic_phase,
     ]
-    full, *sends = call(
-        pack,
-        [sds(planes, tiles, total, LANES)]
-        + [sds(packed, columns)] * 2
+    hbm = lambda v: pltpu.with_memory_space_constraint(v, pltpu.HBM)
+    field = hbm(initial_guess_field)
+    label = hbm(medium_label)
+    near_x, far_x = call(
+        pack_rows,
+        [sds(packed, columns)] * 2,
+        [HBM] * 2,
+        [VMEM] * 2,
+        [
+            pltpu.VMEM((2 * points, 2, STRIP, columns), F32),
+            pltpu.VMEM((2, STRIP, columns), jnp.int32),
+            pltpu.SemaphoreType.DMA((2 * planes,)),
+        ],
+        limit=8,
+    )(field, label)
+
+    def send(value, axis, pairs):
+        return lax.ppermute(value, axis, pairs(axis))
+
+    far_x = send(far_x, "gx", swap_far)
+    near_x = send(near_x, "gx", swap_near)
+    full, near_y, far_y, *small = call(
+        load,
+        [sds(planes, tiles, rows, LANES)]
         + [sds(rows, LANES)] * 2
         + [sds(*value.shape) for value in small],
         [HBM] * 9,
-        [VMEM] * 12,
+        [VMEM] * 10,
         [
             pltpu.VMEM((tiles, rows, LANES), jnp.int32),
             pltpu.SemaphoreType.DMA((tiles * planes + len(small),)),
         ],
         limit=8,
-    )(*[pltpu.with_memory_space_constraint(v, pltpu.HBM) for v in (initial_guess_field, medium_label, *small)])
-    near_x, far_x, near_y, far_y, *small = sends
-
-    def send(value, axis, pairs):
-        return lax.ppermute(value, axis, pairs(axis))
-
-    far_x = send(far_x, "gx", swap_far)
-    near_x = send(near_x, "gx", swap_near)
+    )(field, label, *[hbm(v) for v in small])
     far_y = send(far_y, "gy", swap_far)
     near_y = send(near_y, "gy", swap_near)
 
@@ -729,12 +770,14 @@
         finish,
         [sds(points, STEPS, 2 * rows, columns), sds(points, STEPS, 2, names)],
         [VMEM] * 5,
-        [ANY, VMEM],
+        [ANY, ANY],
         [
-            pltpu.VMEM((STEPS, tiles, 2 * rows, LANES), F32),
-            pltpu.VMEM((STEPS, columns, LANES), F32),
+            pltpu.VMEM((points, STEPS, tiles, 2 * rows, LANES), F32),
+            pltpu.VMEM((points, STEPS, columns, LANES), F32),
             pltpu.VMEM((points, STEPS, 2 * rows, columns), F32),
-            pltpu.SemaphoreType.DMA((points, STEPS)),
+            pltpu.VMEM((points, STEPS, 2, names), F32),
+            pltpu.SemaphoreType.DMA((points, STEPS, 2 * rows // 32)),
+            pltpu.SemaphoreType.DMA,
         ],
         limit=16,
     )(own, out, part, chain, size)

time: 36.6 us -> 35.1 us (0.959)
  waiting for transfers between devices: 2.47 us -> 0.93 us
    ppermute x6, waiting for transfers between devices: 2.47 us -> 0.93 us  [send(): return lax.ppermute(value, axis, pairs(axis))]
    pallas_call x1, Pallas kernels: 3.53 us -> 2.38 us  [per_device(): call(finish, [sds(points, STEPS, 2 * rows, columns), sds(points, STEPS, 2...]
    pallas_call x1 -> x2, Pallas kernels: 1.49 us -> 2.5 us  [the longest x1 1.46 us: per_device(): call(load, [sds(planes, tiles, rows, LANES)] + [sds(rows, LANES)] * 2 + [...]
  transfers between devices with their start and end apart: 6 -> 6, of which waited for: 2 -> 1; matrix products, arithmetic and copies ran while one was open for 0% -> 0% of each run, Pallas kernels for 7% -> 11%
where the time goes in v4:
time: 35.1 us; the launch traced here: 34.8 us
  Pallas kernels  12.1 us (34%)
  blocking collectives  11 us (31%)
  starting transfers between devices  9.99 us (28%)
  waiting for transfers between devices  0.93 us (3%)
  between operations  0.73 us (2%)
    all_to_all x1, blocking collectives, per_device(): part = lax.all_to_all(gram, ('gx', 'gy'), 0, 0, tiled=True)  11 us
    ppermute x6, starting transfers between devices, send(): return lax.ppermute(value, axis, pairs(axis))  9.99 us
    pallas_call x1, Pallas kernels, per_device(): call(solve, [sds(STEPS, points, 2, tiles, total, LANES), sds(devices, 1,...  4.71 us
    pallas_call x1, Pallas kernels, per_device(): call(finish, [sds(points, STEPS, 2 * rows, columns), sds(points, STEPS, 2...  2.38 us
    pallas_call x1, Pallas kernels, per_device(): call(load, [sds(planes, tiles, rows, LANES)] + [sds(rows, LANES)] * 2 + [...  1.46 us
    pallas_call x1, Pallas kernels, per_device(): call(spread, sds(planes, tiles, rows, LANES), [VMEM], VMEM, limit=4)(full)  1.25 us
    pallas_call x1, Pallas kernels, per_device(): call(pack_rows, [sds(packed, columns)] * 2, [HBM] * 2, [VMEM] * 2, [pltpu...  1.04 us
    ppermute x6, waiting for transfers between devices, send(): return lax.ppermute(value, axis, pairs(axis))  0.93 us
  transfers between devices with their start and end apart: 6, of which 1 were waited for; matrix products, arithmetic and copies ran while one was open for 0% of the time, Pallas kernels for 11%

profile of v4, /device:TPU:0, one launch (start us, length us, event | category | flops | bytes accessed | tf_op | source)
XLA Modules:
  0.0 34.8 jit_solution(7524557882431889455)
XLA Ops:
  0.6 1.0 %shard_map.106 = (f32[64,512]{1,0:T(8,128)S(1)}, f32[64,512]{1,0:T(8,128)S(1)}) custom-call(f32[2,2,64,512]{3,2,1,0:T(8,128)} %z_hbm.3, s32[64,512]{1,0:T(8,128)} %m_hbm.3), custom_call_target="tpu_custom_call" | custom-call | tf_op jit(solution)/shard_map/pallas_call | solution.py:679
  1.7 3.0 %collective-permute-start.2 = (f32[64,512]{1,0:T(8,128)S(1)}, f32[64,512]{1,0:T(8,128)S(1)}, u32[]{:S(2)}, u32[]{:S(2)}) collective-permute-start(f32[64,512]{1,0:T(8,128)S(1)} %get-tuple-element.29), channel_id=1, source_target_pairs={{0,4},{4,0},{8,12},{12,8},{16,20},{20,16},{24,28},{28,24},{1,5},{5... | collective-permute-start | bytes 393224 | tf_op jit(solution)/shard_map/ppermute | solution.py:693
  4.7 3.6 %collective-permute-start.3 = (f32[64,512]{1,0:T(8,128)S(1)}, f32[64,512]{1,0:T(8,128)S(1)}, u32[]{:S(2)}, u32[]{:S(2)}) collective-permute-start(f32[64,512]{1,0:T(8,128)S(1)} %get-tuple-element.30), channel_id=1, source_target_pairs={{0,28},{4,8},{8,4},{12,16},{16,12},{20,24},{24,20},{28,0},{1,29},{... | collective-permute-start | bytes 393224 | tf_op jit(solution)/shard_map/ppermute | solution.py:693
  8.3 1.5 %shard_map.104 = (f32[5,4,64,128]{3,2,1,0:T(8,128)S(1)}, f32[64,128]{1,0:T(8,128)S(1)}, f32[64,128]{1,0:T(8,128)S(1)}, f32[2,4]{1,0:T(2,128)S(1)}, f32[4,2,25]{2...) custom-call(f32[2,2,64,512]{3,2,1,0:T(8,128)} %z_hbm.3, ...), custom_call_target="tpu_custom_call" | custom-call | tf_op jit(solution)/shard_map/pallas_call | solution.py:697
  9.8 0.1 collective-permute-start
  9.8 1.6 %collective-permute-start.1 = (f32[64,128]{1,0:T(8,128)S(1)}, f32[64,128]{1,0:T(8,128)S(1)}, u32[]{:S(2)}, u32[]{:S(2)}) collective-permute-start(f32[64,128]{1,0:T(8,128)S(1)} %get-tuple-element.28), channel_id=1, source_target_pairs={{0,3},{1,2},{2,1},{3,0},{4,7},{5,6},{6,5},{7,4},{8,11},{9,10},{10,... | collective-permute-start | bytes 98312 | tf_op jit(solution)/shard_map/ppermute | solution.py:693
  11.5 0.0 collective-permute-done.2.near_x
  11.5 0.9 %collective-permute-done.3.far_x = f32[64,512]{1,0:T(8,128)S(1)} collective-permute-done((f32[64,512]{1,0:T(8,128)S(1)}, f32[64,512]{1,0:T(8,128)S(1)}, u32[]{:S(2)}, u32[]{:S(2)}) %collective-permute-start.3) | collective-permute-done | bytes 131104 | tf_op jit(solution)/shard_map/ppermute | solution.py:693
  12.4 0.1 shard_map.107
  12.5 0.1 collective-permute-start.4
  12.6 1.6 %collective-permute-start.5 = (f32[24,128]{1,0:T(8,128)S(1)}, f32[24,128]{1,0:T(8,128)S(1)}, u32[]{:S(2)}, u32[]{:S(2)}) collective-permute-start(f32[24,128]{1,0:T(8,128)S(1)} %get-tuple-element.32), channel_id=1, source_target_pairs={{0,3},{1,2},{2,1},{3,0},{4,7},{5,6},{6,5},{7,4},{8,11},{9,10},{10,... | collective-permute-start | bytes 36872 | tf_op jit(solution)/shard_map/ppermute | solution.py:693
  14.2 1.3 %shard_map.105.own_ref = f32[5,4,64,128]{3,2,1,0:T(8,128)S(1)} custom-call(f32[5,4,64,128]{3,2,1,0:T(8,128)S(1)} %get-tuple-element.26.full_ref), custom_call_target="tpu_custom_call" | custom-call | tf_op jit(solution)/shard_map/pallas_call | solution.py:726
  15.5 0.4 %shard_map.108 = (f32[8,4,8,128]{3,2,1,0:T(8,128)S(1)}, f32[2,2,2,8,128]{4,3,2,1,0:T(8,128)S(1)}, f32[5,2,32,128]{3,2,1,0:T(8,128)S(1)}, f32[8,128]{1,0:T(8,128)S(1)}) custom-call(f32[2,4]{1,0:T(2,128)S(1)} %get-tuple-element.33.a_ref, f32[4,2,25]{2,1,0:T(2,128)S(1)} %get-tuple-element.34.w_ref, f32[2,24]{1,0:T(2,128)S(1)} %get-tuple-element.35.node_ref, ...), custom_call_target="tpu_custom_call" | custom-call | tf_op jit(solution)/shard_map/pallas_call | solution.py:713
  15.8 0.8 %shard_map.109 = (f32[6,4,11,8,128]{4,3,2,1,0:T(8,128)S(1)}, f32[2,2,4,11,8,128]{5,4,3,2,1,0:T(8,128)S(1)}) custom-call(f32[5,4,64,128]{3,2,1,0:T(8,128)S(1)} %shard_map.105.own_ref, f32[64,512]{1,0:T(8,128)S(1)} %collective-permute-done.2.near_x, f32[64,512]{1,0:T(8,128)S(1)} %collective-permute-done.3.far_x, ...), custom_call_target="tpu_custom_call" | custom-call | tf_op jit(solution)/shard_map/pallas_call | solution.py:740
  16.6 0.0 collective-permute-done.near_y
  16.6 0.0 collective-permute-done.1.far_y
  16.6 0.0 collective-permute-done.4.near_c
  16.6 0.0 collective-permute-done.5.far_c
  16.7 4.7 %shard_map.110 = (f32[3,2,2,4,88,128]{5,4,3,2,1,0:T(8,128)S(1)}, f32[32,1,128]{2,1,0:T(1,128)S(1)}) custom-call(f32[5,4,64,128]{3,2,1,0:T(8,128)S(1)} %shard_map.105.own_ref, f32[64,128]{1,0:T(8,128)S(1)} %collective-permute-done.near_y, f32[64,128]{1,0:T(8,128)S(1)} %collective-permute-done.1.far_y, f32[24,128]{1,0:T(8,128)S(1)} %collective-permute-done.4.near_c, ...), custom_call_target="tpu_custom_call" | custom-call | tf_op jit(solution)/shard_map/pallas_call | solution.py:753
  21.4 11.0 %all_to_all.5.part_ref = f32[32,1,128]{2,1,0:T(1,128)S(1)} all-to-all(f32[32,1,128]{2,1,0:T(1,128)S(1)} %get-tuple-element.45), channel_id=1, replica_groups=mesh['gx'=8,'gy'=4] {'gx','gy'}, dimensions={0} | all-to-all | bytes 32768 | tf_op jit(solution)/shard_map/all_to_all | solution.py:767
  32.4 2.4 %shard_map.111 = (f32[2,3,128,512]{3,2,1,0:T(8,128)}, f32[2,3,2,4]{3,2,1,0:T(2,128)}) custom-call(f32[5,4,64,128]{3,2,1,0:T(8,128)S(1)} %shard_map.105.own_ref, f32[3,2,2,4,88,128]{5,4,3,2,1,0:T(8,128)S(1)} %get-tuple-element.44.out_ref, f32[32,1,128]{2,1,0:T(1,128)S(1)} %all_to_all.5.part_ref, f32[5,2,32,128]{3,2,1,0:T(8,128)S(1)} %get-tuple-element.46.chain_ref, ...), custom_call_target="tpu_custom_call" | custom-call | tf_op jit(solution)/shard_map/pallas_call | solution.py:769
Async XLA Ops:
  1.7 9.8 %collective-permute-start.2 = (f32[64,512]{1,0:T(8,128)S(1)}, f32[64,512]{1,0:T(8,128)S(1)}, u32[]{:S(2)}, u32[]{:S(2)}) collective-permute-start(f32[64,512]{1,0:T(8,128)S(1)} %get-tuple-element.29), channel_id=1, source_target_pairs={{0,4},{4,0},{8,12},{12,8},{16,20},{20,16},{24,28},{28,24},{1,5},{5... | collective-permute-start | bytes 393224 | tf_op jit(solution)/shard_map/ppermute | solution.py:693
  4.7 7.7 %collective-permute-start.3 = (f32[64,512]{1,0:T(8,128)S(1)}, f32[64,512]{1,0:T(8,128)S(1)}, u32[]{:S(2)}, u32[]{:S(2)}) collective-permute-start(f32[64,512]{1,0:T(8,128)S(1)} %get-tuple-element.30), channel_id=1, source_target_pairs={{0,28},{4,8},{8,4},{12,16},{16,12},{20,24},{24,20},{28,0},{1,29},{... | collective-permute-start | bytes 393224 | tf_op jit(solution)/shard_map/ppermute | solution.py:693
  9.8 6.9 %collective-permute-start = (f32[64,128]{1,0:T(8,128)S(1)}, f32[64,128]{1,0:T(8,128)S(1)}, u32[]{:S(2)}, u32[]{:S(2)}) collective-permute-start(f32[64,128]{1,0:T(8,128)S(1)} %get-tuple-element.27), channel_id=1, source_target_pairs={{0,1},{1,0},{2,3},{3,2},{4,5},{5,4},{6,7},{7,6},{8,9},{9,8},{10,11... | collective-permute-start | bytes 98312 | tf_op jit(solution)/shard_map/ppermute | solution.py:693
  9.8 6.8 %collective-permute-start.1 = (f32[64,128]{1,0:T(8,128)S(1)}, f32[64,128]{1,0:T(8,128)S(1)}, u32[]{:S(2)}, u32[]{:S(2)}) collective-permute-start(f32[64,128]{1,0:T(8,128)S(1)} %get-tuple-element.28), channel_id=1, source_target_pairs={{0,3},{1,2},{2,1},{3,0},{4,7},{5,6},{6,5},{7,4},{8,11},{9,10},{10,... | collective-permute-start | bytes 98312 | tf_op jit(solution)/shard_map/ppermute | solution.py:693
  12.5 4.1 %collective-permute-start.4 = (f32[24,128]{1,0:T(8,128)S(1)}, f32[24,128]{1,0:T(8,128)S(1)}, u32[]{:S(2)}, u32[]{:S(2)}) collective-permute-start(f32[24,128]{1,0:T(8,128)S(1)} %get-tuple-element.31), channel_id=1, source_target_pairs={{0,1},{1,0},{2,3},{3,2},{4,5},{5,4},{6,7},{7,6},{8,9},{9,8},{10,11... | collective-permute-start | bytes 36872 | tf_op jit(solution)/shard_map/ppermute | solution.py:693
  12.6 4.1 %collective-permute-start.5 = (f32[24,128]{1,0:T(8,128)S(1)}, f32[24,128]{1,0:T(8,128)S(1)}, u32[]{:S(2)}, u32[]{:S(2)}) collective-permute-start(f32[24,128]{1,0:T(8,128)S(1)} %get-tuple-element.32), channel_id=1, source_target_pairs={{0,3},{1,2},{2,1},{3,0},{4,7},{5,6},{6,5},{7,4},{8,11},{9,10},{10,... | collective-permute-start | bytes 36872 | tf_op jit(solution)/shard_map/ppermute | solution.py:693

commit v5 on v4

--- a/solution.py
+++ b/solution.py
@@ -262,7 +262,30 @@
     return co, jnp.where(edge, jnp.where(low, sine, -sine), 0.0)
 
 
-def stage(own_ref, near_x, far_x, table_ref, trig_ref, cell_ref, b_ref, raw_ref, work_ref):
+def column_halo(near, far, trig_ref, planes):
+    y_even = even("gy")
+    right_src = jnp.where(y_even, near, far)
+    left_src = jnp.where(y_even, far, near)
+    lane = lax.broadcasted_iota(jnp.int32, near.shape, 1)
+    is_right = lane < HALO
+    is_left = lane >= LANES - HALO
+    values = []
+    for plane in range(planes):
+        right = pltpu.roll(right_src, (LANES - plane * SLOT) % LANES, 1)
+        left = pltpu.roll(left_src, (LANES - HALO - plane * SLOT) % LANES, 1)
+        values.append(jnp.where(is_right, right, jnp.where(is_left, left, 0.0)))
+    first, last = ends("gy")
+    edge = jnp.where(is_right, last, jnp.where(is_left, first, 0.0)) > 0.5
+    for k in range(planes // 2):
+        sine = trig_ref[k, 1, 1][0:1, :]
+        co = jnp.where(edge, trig_ref[k, 1, 0][0:1, :], 1.0)
+        si = jnp.where(edge, jnp.where(is_right, sine, -sine), 0.0)
+        values[2 * k : 2 * k + 2] = cmul(values[2 * k : 2 * k + 2], (co, si))
+    return values
+
+
+def stage(own_ref, near_x, far_x, near_y, far_y, table_ref, trig_ref,
+          cell_ref, b_ref, side_ref, raw_ref, work_ref):
     planes, tiles, rows, _ = own_ref.shape
     points = planes // 2
     total = rows + 2 * HALO
@@ -288,6 +311,8 @@
             values = spread_lanes([raw_ref[plane, t, r : r + SUB, :] for t in range(tiles)])
             for j, value in enumerate(values):
                 work_ref[plane, j, rows + r : rows + r + SUB, :] = value
+    for plane, value in enumerate(column_halo(near_y[...], far_y[...], trig_ref, planes)):
+        side_ref[plane] = value
     for j in range(tiles):
         for v in range(count):
             span = pl.ds(v, SUB, stride=count)
@@ -301,41 +326,18 @@
                     b_ref[k, c, j, v] = value
 
 
-def solve(own_ref, near_y, far_y, near_c, far_c, table_ref, trig_ref, cell_own, b_own,
-          out_ref, gram_ref, edge_ref, halo_ref, cell_halo, b_ref, x_ref, w_ref, keep_ref):
+def solve(own_ref, side_ref, near_c, far_c, table_ref, trig_ref, cell_own, b_own,
+          out_ref, gram_ref, halo_ref, cell_halo, b_ref, x_ref, w_ref, keep_ref):
     planes, tiles, rows, _ = own_ref.shape
     points = planes // 2
     total = rows + 2 * HALO
     count = total // SUB
-    y_even = even("gy")
-    for side in range(2):
-        keep = y_even if side == 0 else jnp.logical_not(y_even)
-        edge_ref[side, 0:rows, :] = jnp.where(keep, near_y[...], far_y[...])
-        edge_ref[side, rows:total, :] = jnp.where(keep, near_c[...], far_c[...])
-    lane = lax.broadcasted_iota(jnp.int32, (total, LANES), 1)
-    is_right = lane < HALO
-    is_left = lane >= LANES - HALO
-    right_src = edge_ref[0]
-    left_src = edge_ref[1]
+    corner = column_halo(near_c[...], far_c[...], trig_ref, planes)
+    for k in range(points):
+        corner[2 * k : 2 * k + 2] = cmul(corner[2 * k : 2 * k + 2], row_turns(trig_ref, k))
     for plane in range(planes):
-        right = pltpu.roll(right_src, (LANES - plane * SLOT) % LANES, 1)
-        left = pltpu.roll(left_src, (LANES - HALO - plane * SLOT) % LANES, 1)
-        halo_ref[plane] = jnp.where(is_right, right, jnp.where(is_left, left, 0.0))
-    first, last = ends("gy")
-    y_edge = jnp.where(is_right, last, jnp.where(is_left, first, 0.0)) > 0.5
-    for k in range(points):
-        turned = cmul(
-            (halo_ref[2 * k, rows:total, :], halo_ref[2 * k + 1, rows:total, :]),
-            row_turns(trig_ref, k),
-        )
-        halo_ref[2 * k, rows:total, :] = turned[0]
-        halo_ref[2 * k + 1, rows:total, :] = turned[1]
-        sine = trig_ref[k, 1, 1][0:1, :]
-        co = jnp.where(y_edge, trig_ref[k, 1, 0][0:1, :], 1.0)
-        si = jnp.where(y_edge, jnp.where(is_right, sine, -sine), 0.0)
-        turned = cmul((halo_ref[2 * k], halo_ref[2 * k + 1]), (co, si))
-        halo_ref[2 * k] = turned[0]
-        halo_ref[2 * k + 1] = turned[1]
+        halo_ref[plane, 0:rows, :] = side_ref[plane]
+        halo_ref[plane, rows:total, :] = corner[plane]
     for v in range(count):
         span = pl.ds(v, SUB, stride=count)
         pick = picker(halo_ref[planes - 1, span, :], table_ref)
@@ -346,11 +348,6 @@
             z = (halo_ref[2 * k, span, :], halo_ref[2 * k + 1, span, :])
             for c, value in enumerate(cmul(weight, z)):
                 b_ref[k, c, tiles, v] = value
-                x_ref[k, c, tiles, v] = value
-                for t in range(tiles):
-                    own = b_own[k, c, t, v]
-                    b_ref[k, c, t, v] = own
-                    x_ref[k, c, t, v] = own
 
     def cell(e, t, v):
         return cell_own[e, t, v] if t < tiles else cell_halo[e, v]
@@ -359,63 +356,76 @@
     at_first = lane8 == 0
     at_last = lane8 == LANES - 1
 
-    def sweep(src_ref, dst_ref):
-        for k in range(points):
-            for v in range(count):
-                sides = []
+    def sweep(src, right_side, dst_ref):
+        held = {}
+        for k, v in [(k, v) for v in range(count) for k in range(points)]:
+                sums = []
                 for c in range(2):
-                    x = [src_ref[k, c, t, v] for t in range(tiles + 1)]
+                    x = [src(k, c, t, v) for t in range(tiles + 1)]
                     last_on = pltpu.roll(x[tiles - 1], 1, 1)
                     halo_on = pltpu.roll(x[tiles], 1, 1)
                     first_back = pltpu.roll(x[0], LANES - 1, 1)
                     halo_back = pltpu.roll(x[tiles], LANES - 1, 1)
                     left = [jnp.where(at_first, halo_on, last_on)] + x[: tiles - 1]
                     right = x[1:tiles] + [jnp.where(at_last, halo_back, first_back)]
-                    side = [a + b for a, b in zip(left, right)]
-                    one = jnp.where(at_first, last_on, halo_on)
-                    two = jnp.where(at_last, first_back, halo_back)
-                    sides.append(side + [one + two])
+                    left.append(jnp.where(at_first, last_on, halo_on))
+                    right.append(jnp.where(at_last, first_back, halo_back))
+                    before = held.get((k, c))
+                    after = []
+                    total_n = []
+                    for t in range(tiles + 1):
+                        if v < count - 1:
+                            down = src(k, c, t, v + 1)
+                        else:
+                            down = pltpu.roll(src(k, c, t, 0), SUB - 1, 0)
+                        after.append(right[t] + down)
+                        if before is not None and 0 < t < tiles:
+                            other = before[t - 1]
+                        elif v > 0:
+                            other = left[t] + src(k, c, t, v - 1)
+                        else:
+                            other = left[t] + pltpu.roll(src(k, c, t, count - 1), 1, 0)
+                        total_n.append(other + after[t])
+                    held[k, c] = after
+                    sums.append(total_n)
                 for t in range(tiles + 1):
-                    n = []
+                    n = cmul((cell(0, t, v), cell(1, t, v)), (sums[0][t], sums[1][t]))
                     for c in range(2):
-                        if v > 0:
-                            up = src_ref[k, c, t, v - 1]
-                        else:
-                            up = pltpu.roll(src_ref[k, c, t, count - 1], 1, 0)
-                        if v < count - 1:
-                            down = src_ref[k, c, t, v + 1]
-                        else:
-                            down = pltpu.roll(src_ref[k, c, t, 0], SUB - 1, 0)
-                        n.append(sides[c][t] + (up + down))
-                    n = cmul((cell(0, t, v), cell(1, t, v)), n)
-                    for c in range(2):
-                        dst_ref[k, c, t, v] = b_ref[k, c, t, v] + n[c]
-
-    def pair(i, carry):
-        sweep(x_ref, w_ref)
-        sweep(w_ref, x_ref)
-        return carry
+                        dst_ref[k, c, t, v] = right_side(k, c, t, v) + n[c]
+
+    def reader(ref):
+        return lambda *at: ref[at]
+
+    def first_side(k, c, t, v):
+        return b_own[k, c, t, v] if t < tiles else b_ref[k, c, t, v]
 
     for s in range(STEPS):
-        lax.fori_loop(0, SWEEPS // 2, pair, 0)
+        right_side = reader(b_ref) if s else first_side
+        sweep(right_side, right_side, w_ref)
+        sweep(reader(w_ref), right_side, x_ref)
+        for _ in range(SWEEPS // 2 - 1):
+            sweep(reader(x_ref), right_side, w_ref)
+            sweep(reader(w_ref), right_side, x_ref)
         for k in range(points):
             for t in range(tiles + 1):
                 for v in range(count):
+                    span = pl.ds(v, SUB, stride=count)
                     y = (x_ref[k, 0, t, v], x_ref[k, 1, t, v])
-                    if t < tiles:
-                        for c in range(2):
-                            out_ref[s, k, c, t, pl.ds(v, SUB, stride=count), :] = y[c]
+                    for c in range(2):
+                        if t < tiles:
+                            out_ref[s, k, c, t, span, :] = y[c]
+                        elif s == 0:
+                            keep_ref[k, c, v] = y[c]
                     if s < STEPS - 1:
                         b = cmul((cell(2, t, v), cell(3, t, v)), y)
-                        if s == 0:
-                            keep = cmul((cell(4, t, v), cell(5, t, v)), y)
-                            for c in range(2):
-                                keep_ref[k, c, t, v] = keep[c]
-                        else:
-                            b = cadd(b, (keep_ref[k, 0, t, v], keep_ref[k, 1, t, v]))
+                        if s == 1:
+                            if t < tiles:
+                                old = (out_ref[0, k, 0, t, span, :], out_ref[0, k, 1, t, span, :])
+                            else:
+                                old = (keep_ref[k, 0, v], keep_ref[k, 1, v])
+                            b = cadd(b, cmul((cell(4, t, v), cell(5, t, v)), old))
                         for c in range(2):
                             b_ref[k, c, t, v] = b[c]
-                            x_ref[k, c, t, v] = b[c]
 
     names = STEPS + 1
     zero = jnp.zeros((SUB, LANES), F32)
@@ -737,32 +747,32 @@
     near_c = send(near_c, "gy", swap_near)
 
     narrow = (tiles, count, SUB, LANES)
-    cell, b = call(
+    cell, b, side = call(
         stage,
-        [sds(6, *narrow), sds(points, 2, *narrow)],
-        [VMEM] * 5,
-        [VMEM] * 2,
+        [sds(6, *narrow), sds(points, 2, *narrow), sds(planes, rows, LANES)],
+        [VMEM] * 7,
+        [VMEM] * 3,
         [
             pltpu.VMEM((planes, tiles, 2 * HALO, LANES), F32),
             pltpu.VMEM((planes, tiles, total, LANES), F32),
         ],
         limit=8,
-    )(own, near_x, far_x, table, trig)
+    )(own, near_x, far_x, near_y, far_y, table, trig)
 
     wide = (tiles + 1, count, SUB, LANES)
     out, gram = call(
         solve,
         [sds(STEPS, points, 2, tiles, total, LANES), sds(devices, 1, LANES)],
-        [VMEM] * 9,
+        [VMEM] * 8,
         [VMEM] * 2,
         [
-            pltpu.VMEM((2, total, LANES), F32),
             pltpu.VMEM((planes, total, LANES), F32),
             pltpu.VMEM((6,) + wide[1:], F32),
         ]
-        + [pltpu.VMEM((points, 2) + wide, F32)] * 4,
+        + [pltpu.VMEM((points, 2) + wide, F32)] * 3
+        + [pltpu.VMEM((points, 2) + wide[1:], F32)],
         limit=32,
-    )(own, near_y, far_y, near_c, far_c, table, trig, cell, b)
+    )(own, side, near_c, far_c, table, trig, cell, b)
 
     part = lax.all_to_all(gram, ("gx", "gy"), 0, 0, tiled=True)
 

time: 35.1 us -> 34.8 us (level)
  transfers between devices with their start and end apart: 6 -> 6, of which waited for: 1 -> 1; matrix products, arithmetic and copies ran while one was open for 0% -> 0% of each run, Pallas kernels for 11% -> 12%
where the time goes in v5:
time: 34.8 us; the launch traced here: 34.5 us
  Pallas kernels  11.8 us (34%)
  blocking collectives  11 us (32%)
  starting transfers between devices  9.99 us (29%)
  waiting for transfers between devices  0.93 us (3%)
  between operations  0.73 us (2%)
    all_to_all x1, blocking collectives, per_device(): part = lax.all_to_all(gram, ('gx', 'gy'), 0, 0, tiled=True)  11 us
    ppermute x6, starting transfers between devices, send(): return lax.ppermute(value, axis, pairs(axis))  9.99 us
    pallas_call x1, Pallas kernels, per_device(): call(solve, [sds(STEPS, points, 2, tiles, total, LANES), sds(devices, 1,...  4.4 us
    pallas_call x1, Pallas kernels, per_device(): call(finish, [sds(points, STEPS, 2 * rows, columns), sds(points, STEPS, 2...  2.38 us
    pallas_call x1, Pallas kernels, per_device(): call(load, [sds(planes, tiles, rows, LANES)] + [sds(rows, LANES)] * 2 + [...  1.46 us
    pallas_call x1, Pallas kernels, per_device(): call(spread, sds(planes, tiles, rows, LANES), [VMEM], VMEM, limit=4)(full)  1.25 us
    pallas_call x1, Pallas kernels, per_device(): call(pack_rows, [sds(packed, columns)] * 2, [HBM] * 2, [VMEM] * 2, [pltpu...  1.04 us
    ppermute x6, waiting for transfers between devices, send(): return lax.ppermute(value, axis, pairs(axis))  0.93 us
  transfers between devices with their start and end apart: 6, of which 1 were waited for; matrix products, arithmetic and copies ran while one was open for 0% of the time, Pallas kernels for 12%

profile of v5, /device:TPU:0, one launch (start us, length us, event | category | flops | bytes accessed | tf_op | source)
XLA Modules:
  0.0 34.5 jit_solution(407333217835083735)
XLA Ops:
  0.6 1.0 %shard_map.106 = (f32[64,512]{1,0:T(8,128)S(1)}, f32[64,512]{1,0:T(8,128)S(1)}) custom-call(f32[2,2,64,512]{3,2,1,0:T(8,128)} %z_hbm.3, s32[64,512]{1,0:T(8,128)} %m_hbm.3), custom_call_target="tpu_custom_call" | custom-call | tf_op jit(solution)/shard_map/pallas_call | solution.py:689
  1.7 3.0 %collective-permute-start = (f32[64,512]{1,0:T(8,128)S(1)}, f32[64,512]{1,0:T(8,128)S(1)}, u32[]{:S(2)}, u32[]{:S(2)}) collective-permute-start(f32[64,512]{1,0:T(8,128)S(1)} %get-tuple-element.28), channel_id=1, source_target_pairs={{0,4},{4,0},{8,12},{12,8},{16,20},{20,16},{24,28},{28,24},{1,5},{5... | collective-permute-start | bytes 393224 | tf_op jit(solution)/shard_map/ppermute | solution.py:703
  4.7 3.6 %collective-permute-start.1 = (f32[64,512]{1,0:T(8,128)S(1)}, f32[64,512]{1,0:T(8,128)S(1)}, u32[]{:S(2)}, u32[]{:S(2)}) collective-permute-start(f32[64,512]{1,0:T(8,128)S(1)} %get-tuple-element.29), channel_id=1, source_target_pairs={{0,28},{4,8},{8,4},{12,16},{16,12},{20,24},{24,20},{28,0},{1,29},{... | collective-permute-start | bytes 393224 | tf_op jit(solution)/shard_map/ppermute | solution.py:703
  8.3 1.5 %shard_map.104 = (f32[5,4,64,128]{3,2,1,0:T(8,128)S(1)}, f32[64,128]{1,0:T(8,128)S(1)}, f32[64,128]{1,0:T(8,128)S(1)}, f32[2,4]{1,0:T(2,128)S(1)}, f32[4,2,25]{2...) custom-call(f32[2,2,64,512]{3,2,1,0:T(8,128)} %z_hbm.3, ...), custom_call_target="tpu_custom_call" | custom-call | tf_op jit(solution)/shard_map/pallas_call | solution.py:707
  9.8 0.1 collective-permute-start.2
  9.8 1.6 %collective-permute-start.3 = (f32[64,128]{1,0:T(8,128)S(1)}, f32[64,128]{1,0:T(8,128)S(1)}, u32[]{:S(2)}, u32[]{:S(2)}) collective-permute-start(f32[64,128]{1,0:T(8,128)S(1)} %get-tuple-element.31), channel_id=1, source_target_pairs={{0,3},{1,2},{2,1},{3,0},{4,7},{5,6},{6,5},{7,4},{8,11},{9,10},{10,... | collective-permute-start | bytes 98312 | tf_op jit(solution)/shard_map/ppermute | solution.py:703
  11.5 0.0 collective-permute-done.near_x
  11.5 0.9 %collective-permute-done.1.far_x = f32[64,512]{1,0:T(8,128)S(1)} collective-permute-done((f32[64,512]{1,0:T(8,128)S(1)}, f32[64,512]{1,0:T(8,128)S(1)}, u32[]{:S(2)}, u32[]{:S(2)}) %collective-permute-start.1) | collective-permute-done | bytes 131104 | tf_op jit(solution)/shard_map/ppermute | solution.py:703
  12.4 0.1 shard_map.109
  12.5 0.1 collective-permute-start.4
  12.6 1.6 %collective-permute-start.5 = (f32[24,128]{1,0:T(8,128)S(1)}, f32[24,128]{1,0:T(8,128)S(1)}, u32[]{:S(2)}, u32[]{:S(2)}) collective-permute-start(f32[24,128]{1,0:T(8,128)S(1)} %get-tuple-element.43), channel_id=1, source_target_pairs={{0,3},{1,2},{2,1},{3,0},{4,7},{5,6},{6,5},{7,4},{8,11},{9,10},{10,... | collective-permute-start | bytes 36872 | tf_op jit(solution)/shard_map/ppermute | solution.py:703
  14.2 1.3 %shard_map.105.own_ref = f32[5,4,64,128]{3,2,1,0:T(8,128)S(1)} custom-call(f32[5,4,64,128]{3,2,1,0:T(8,128)S(1)} %get-tuple-element.27.full_ref), custom_call_target="tpu_custom_call" | custom-call | tf_op jit(solution)/shard_map/pallas_call | solution.py:736
  15.5 0.4 %shard_map.107 = (f32[8,4,8,128]{3,2,1,0:T(8,128)S(1)}, f32[2,2,2,8,128]{4,3,2,1,0:T(8,128)S(1)}, f32[5,2,32,128]{3,2,1,0:T(8,128)S(1)}, f32[8,128]{1,0:T(8,128)S(1)}) custom-call(f32[2,4]{1,0:T(2,128)S(1)} %get-tuple-element.32.a_ref, f32[4,2,25]{2,1,0:T(2,128)S(1)} %get-tuple-element.33.w_ref, f32[2,24]{1,0:T(2,128)S(1)} %get-tuple-element.34.node_ref, ...), custom_call_target="tpu_custom_call" | custom-call | tf_op jit(solution)/shard_map/pallas_call | solution.py:723
  15.8 0.0 collective-permute-done.2.near_y
  15.8 0.0 collective-permute-done.3.far_y
  15.9 0.8 %shard_map.108 = (f32[6,4,11,8,128]{4,3,2,1,0:T(8,128)S(1)}, f32[2,2,4,11,8,128]{5,4,3,2,1,0:T(8,128)S(1)}, f32[5,64,128]{2,1,0:T(8,128)S(1)}) custom-call(f32[5,4,64,128]{3,2,1,0:T(8,128)S(1)} %shard_map.105.own_ref, f32[64,512]{1,0:T(8,128)S(1)} %collective-permute-done.near_x, f32[64,512]{1,0:T(8,128)S(1)} %collective-permute-done.1.far_x, ...), custom_call_target="tpu_custom_call" | custom-call | tf_op jit(solution)/shard_map/pallas_call | solution.py:750
  16.7 0.0 collective-permute-done.4.near_c
  16.7 0.0 collective-permute-done.5.far_c
  16.7 4.4 %shard_map.110 = (f32[3,2,2,4,88,128]{5,4,3,2,1,0:T(8,128)S(1)}, f32[32,1,128]{2,1,0:T(1,128)S(1)}) custom-call(f32[5,4,64,128]{3,2,1,0:T(8,128)S(1)} %shard_map.105.own_ref, f32[5,64,128]{2,1,0:T(8,128)S(1)} %get-tuple-element.41.side_ref, f32[24,128]{1,0:T(8,128)S(1)} %collective-permute-done.4.near_c, f32[24,128]{1,0:T(8,128)S(1)} %collective-permute-done.5.far_c, ...), custom_call_target="tpu_custom_call" | custom-call | tf_op jit(solution)/shard_map/pallas_call | solution.py:763
  21.1 11.0 %all_to_all.5.part_ref = f32[32,1,128]{2,1,0:T(1,128)S(1)} all-to-all(f32[32,1,128]{2,1,0:T(1,128)S(1)} %get-tuple-element.47), channel_id=1, replica_groups=mesh['gx'=8,'gy'=4] {'gx','gy'}, dimensions={0} | all-to-all | bytes 32768 | tf_op jit(solution)/shard_map/all_to_all | solution.py:777
  32.1 2.4 %shard_map.111 = (f32[2,3,128,512]{3,2,1,0:T(8,128)}, f32[2,3,2,4]{3,2,1,0:T(2,128)}) custom-call(f32[5,4,64,128]{3,2,1,0:T(8,128)S(1)} %shard_map.105.own_ref, f32[3,2,2,4,88,128]{5,4,3,2,1,0:T(8,128)S(1)} %get-tuple-element.46.out_ref, f32[32,1,128]{2,1,0:T(1,128)S(1)} %all_to_all.5.part_ref, f32[5,2,32,128]{3,2,1,0:T(8,128)S(1)} %get-tuple-element.48.chain_ref, ...), custom_call_target="tpu_custom_call" | custom-call | tf_op jit(solution)/shard_map/pallas_call | solution.py:779
Async XLA Ops:
  1.7 9.8 %collective-permute-start = (f32[64,512]{1,0:T(8,128)S(1)}, f32[64,512]{1,0:T(8,128)S(1)}, u32[]{:S(2)}, u32[]{:S(2)}) collective-permute-start(f32[64,512]{1,0:T(8,128)S(1)} %get-tuple-element.28), channel_id=1, source_target_pairs={{0,4},{4,0},{8,12},{12,8},{16,20},{20,16},{24,28},{28,24},{1,5},{5... | collective-permute-start | bytes 393224 | tf_op jit(solution)/shard_map/ppermute | solution.py:703
  4.7 7.7 %collective-permute-start.1 = (f32[64,512]{1,0:T(8,128)S(1)}, f32[64,512]{1,0:T(8,128)S(1)}, u32[]{:S(2)}, u32[]{:S(2)}) collective-permute-start(f32[64,512]{1,0:T(8,128)S(1)} %get-tuple-element.29), channel_id=1, source_target_pairs={{0,28},{4,8},{8,4},{12,16},{16,12},{20,24},{24,20},{28,0},{1,29},{... | collective-permute-start | bytes 393224 | tf_op jit(solution)/shard_map/ppermute | solution.py:703
  9.8 6.1 %collective-permute-start.2 = (f32[64,128]{1,0:T(8,128)S(1)}, f32[64,128]{1,0:T(8,128)S(1)}, u32[]{:S(2)}, u32[]{:S(2)}) collective-permute-start(f32[64,128]{1,0:T(8,128)S(1)} %get-tuple-element.30), channel_id=1, source_target_pairs={{0,1},{1,0},{2,3},{3,2},{4,5},{5,4},{6,7},{7,6},{8,9},{9,8},{10,11... | collective-permute-start | bytes 98312 | tf_op jit(solution)/shard_map/ppermute | solution.py:703
  9.8 6.0 %collective-permute-start.3 = (f32[64,128]{1,0:T(8,128)S(1)}, f32[64,128]{1,0:T(8,128)S(1)}, u32[]{:S(2)}, u32[]{:S(2)}) collective-permute-start(f32[64,128]{1,0:T(8,128)S(1)} %get-tuple-element.31), channel_id=1, source_target_pairs={{0,3},{1,2},{2,1},{3,0},{4,7},{5,6},{6,5},{7,4},{8,11},{9,10},{10,... | collective-permute-start | bytes 98312 | tf_op jit(solution)/shard_map/ppermute | solution.py:703
  12.5 4.2 %collective-permute-start.4 = (f32[24,128]{1,0:T(8,128)S(1)}, f32[24,128]{1,0:T(8,128)S(1)}, u32[]{:S(2)}, u32[]{:S(2)}) collective-permute-start(f32[24,128]{1,0:T(8,128)S(1)} %get-tuple-element.42), channel_id=1, source_target_pairs={{0,1},{1,0},{2,3},{3,2},{4,5},{5,4},{6,7},{7,6},{8,9},{9,8},{10,11... | collective-permute-start | bytes 36872 | tf_op jit(solution)/shard_map/ppermute | solution.py:703
  12.6 4.1 %collective-permute-start.5 = (f32[24,128]{1,0:T(8,128)S(1)}, f32[24,128]{1,0:T(8,128)S(1)}, u32[]{:S(2)}, u32[]{:S(2)}) collective-permute-start(f32[24,128]{1,0:T(8,128)S(1)} %get-tuple-element.43), channel_id=1, source_target_pairs={{0,3},{1,2},{2,1},{3,0},{4,7},{5,6},{6,5},{7,4},{8,11},{9,10},{10,... | collective-permute-start | bytes 36872 | tf_op jit(solution)/shard_map/ppermute | solution.py:703
